TPU v7x, 32 devices: a whole 2x2x4 slice. The times are simulated.
32 devices in a mesh: sub: 4 (over x, core), lat: 2 (over y), lon: 4 (over z).
Axes of the slice: x: 2, y: 2, z: 4, core: 2. Of those that a mesh axis runs over, the one named last changes fastest.
Arguments:
- segment_launch_values: float32 [4, 3, 1024, 1024], P('sub', None, 'lat', 'lon'), may hold values from -1.8 to 1.8
- initial_backdrop: float32 [3, 1024, 1024], P(None, 'lat', 'lon'), may hold values from -1.8 to 1.8
- spectral_inverse_variances: float32 [3, 513], replicated, may hold values from 0.3 to 3
Outputs:
- weighted_defects: float32 [4, 3, 1024, 1024], P('sub', None, 'lat', 'lon')
All inputs are finite; a program needn't handle non-finite values.
Results may differ from a plain program's by a relative error of at most 0.00017.
Values sent between devices are 32-bit elements; how exact they have to be, the bound alone decides.
A program may use at most 64 MiB of HBM per device.

v0:
```python
import numpy as np
import jax
import jax.numpy as jnp
from jax import lax
from jax.experimental import pallas as pl
from jax.experimental.pallas import tpu as pltpu
from jax.sharding import PartitionSpec as P

STEPS = 3
HALO = 16
BLOCK = 4
MESH = pl.DeviceIdType.MESH

time_step = 0.5
coriolis_peak = 0.4


def cosine_table(length):
    half = length // 2
    wave = np.arange(half)[:, None]
    angle = (wave * np.arange(length)[None, :]) % length * (2.0 * np.pi / length)
    return (np.where(wave == 0, 1.0, 2.0) / length * np.cos(angle)).astype(np.float32)


def doubled_coriolis(total_rows):
    index = np.arange(total_rows)
    return (2.0 * coriolis_peak * np.sin(2.0 * np.pi * (index + 0.5) / total_rows)).astype(
        np.float32
    )


def split_parts(value):
    high = value.astype(jnp.bfloat16)
    return high, (value - high.astype(jnp.float32)).astype(jnp.bfloat16)


def kernel(
    nsub, nlat, nlon, x_hbm, back_hbm, w_ref, table_hbm, f_smem, out_ref,
    table, wpad, wave_row, conv_hi, conv_lo, frows, slab, fc, state, mid1, mid2,
    prev, y_own, got_own,
    table_sem, main_send, top_send, bot_send, main_recv, top_recv, bot_recv,
    back_send, back_recv, own_send, own_recv, hop_send, hop_recv,
):
    k = lax.axis_index("sub")
    a = lax.axis_index("lat")
    z = lax.axis_index("lon")
    fields, lat_rows, width = x_hbm.shape
    rows = lat_rows // nlon
    total = lat_rows * nlat
    length = width * nlon
    half = length // 2
    lanes = 128
    slices = length // lanes
    padded = rows + 2 * HALO
    k_up = lax.rem(k + 1, nsub)
    k_down = lax.rem(k + nsub - 1, nsub)
    a_up = lax.rem(a + 1, nlat)
    a_down = lax.rem(a + nlat - 1, nlat)
    last = nsub - 1

    barrier = pltpu.get_barrier_semaphore()
    for d in range(1, nlon):
        pl.semaphore_signal(
            barrier, inc=1, device_id=(k, a, lax.rem(z + d, nlon)), device_id_type=MESH
        )
    for d in range(nlon):
        for there in ((k, a_up), (k, a_down), (k_up, a), (k_down, a)):
            pl.semaphore_signal(barrier, inc=1, device_id=there + (jnp.int32(d),), device_id_type=MESH)
    pl.semaphore_wait(barrier, nlon - 1 + 4 * nlon)

    mine = pl.ds(pl.multiple_of(z * width, width), width)

    def local(src, dst, sem):
        return pltpu.make_async_copy(src, dst, sem)

    def remote(src, dst, send, recv, there):
        return pltpu.make_async_remote_copy(
            src_ref=src, dst_ref=dst, send_sem=send, recv_sem=recv,
            device_id=there, device_id_type=MESH,
        )

    def rows_at(first, count):
        return pl.ds(pl.multiple_of(first, 8), count)

    def edge(target, up):
        if up:
            src = x_hbm.at[:, pl.ds(target * rows + rows - HALO, HALO), :]
            dst = slab.at[:, pl.ds(0, HALO), mine]
            lon, lat = (target + 1) % nlon, a_up if target == nlon - 1 else a
            send, recv = top_send.at[target], top_recv.at[z]
        else:
            src = x_hbm.at[:, pl.ds(target * rows, HALO), :]
            dst = slab.at[:, pl.ds(HALO + rows, HALO), mine]
            lon, lat = (target - 1) % nlon, a_down if target == 0 else a
            send, recv = bot_send.at[target], bot_recv.at[z]
        crosses = target == (nlon - 1 if up else 0)
        return src, dst, send, recv, lon, lat, crosses

    def exchange(src_hbm, dst, sends, recvs, first):
        def copy_of(d):
            zt = lax.rem(z + d, nlon)
            src = src_hbm.at[:, rows_at(zt * rows, rows), :]
            into = dst.at[:, pl.ds(first, rows), mine]
            if d == 0:
                return local(src, into, recvs.at[z])
            return remote(src, into, sends.at[d], recvs.at[z], (k, a, zt))

        return [copy_of(d) for d in range(nlon)]

    mains = exchange(x_hbm, slab, main_send, main_recv, HALO)
    for d in (1, nlon - 1) if nlon > 2 else (1,):
        mains[d].start()
    for d in range(2, nlon - 1):
        mains[d].start()
    mains[0].start()
    for up in (True, False):
        for target in range(nlon):
            src, dst, send, recv, lon, lat, crosses = edge(target, up)
            if crosses:
                remote(src, dst, send, recv, (k, lat, jnp.int32(lon))).start()
            else:
                @pl.when(z == lon)
                def _():
                    local(src, dst, recv).start()

                @pl.when(z != lon)
                def _():
                    remote(src, dst, send, recv, (k, lat, jnp.int32(lon))).start()

    table_copy = local(table_hbm, table, table_sem)
    table_copy.start()
    wpad[...] = jnp.zeros_like(wpad)
    wpad[0:fields, 0 : half + 1] = w_ref[...]
    table_copy.wait()
    sign = 1.0 - 2.0 * (lax.broadcasted_iota(jnp.int32, (8, length), 1) % 2).astype(jnp.float32)
    wave_row[...] = (
        jnp.dot(
            wpad[:, 0:half], table[...], precision=lax.Precision.HIGHEST,
            preferred_element_type=jnp.float32,
        )
        + wpad[:, half : half + 1] * (sign / length)
    )
    chunk = 16
    blocks = half // lanes
    for c in range(fields):
        line = 0.5 * wave_row[c : c + 1, :]

        @pl.loop(0, lanes // chunk)
        def _(i):
            row = i * chunk + lax.broadcasted_iota(jnp.int32, (chunk, length), 0)
            turned = jnp.broadcast_to(line, (chunk, length))
            for bit in range(lanes.bit_length() - 1):
                far = pltpu.roll(turned, 1 << bit, 1)
                turned = jnp.where((row >> bit) % 2 == 1, far, turned)
            for q in range(slices):
                first = turned[:, q * lanes : (q + 1) * lanes]
                p = (q + blocks) % slices
                other = turned[:, p * lanes : (p + 1) * lanes]
                for part, value in enumerate((first + other, first - other)):
                    high, low = split_parts(value)
                    for m in range(blocks):
                        t = (q + m) % slices
                        if t < blocks:
                            at = pl.ds(pl.multiple_of(m * lanes + i * chunk, chunk), chunk)
                            conv_hi[2 * c + part, at, t * lanes : (t + 1) * lanes] = high
                            conv_lo[2 * c + part, at, t * lanes : (t + 1) * lanes] = low

    first_row = (a * nlon + z) * rows - HALO + total

    @pl.loop(0, padded)
    def _(r):
        frows[pl.ds(pl.multiple_of(8 * r, 8), 8), :] = jnp.full(
            (8, lanes), f_smem[lax.rem(first_row + r, total)], jnp.float32
        )

    for s in range(nlon):
        cols = pl.ds(s * width, width)
        for first, count, recv in (
            (HALO, rows, main_recv), (0, HALO, top_recv), (HALO + rows, HALO, bot_recv)
        ):
            block = slab.at[:, pl.ds(first, count), cols]
            local(block, block, recv.at[s]).wait()

    backs = exchange(back_hbm, fc, back_send, back_recv, 0)

    @pl.when(k == last)
    def _():
        for d in range(nlon):
            backs[d].start()

    def filtered(c):
        value = slab[c, pl.ds(HALO, rows), :] - prev[c]
        left, right = value[:, :half], value[:, half:]
        halves = []
        for part, mix in enumerate((left + right, left - right)):
            high, low = split_parts(mix)
            both = jnp.concatenate([high, low], axis=0)
            twice = jnp.dot(both, conv_hi[2 * c + part], preferred_element_type=jnp.float32)
            rest = jnp.dot(high, conv_lo[2 * c + part], preferred_element_type=jnp.float32)
            halves.append(twice[:rows] + (twice[rows:] + rest))
        return halves[0] + halves[1], halves[0] - halves[1]

    def home(c, d):
        zt = lax.rem(z + d, nlon)
        src = y_own.at[c, :, pl.ds(pl.multiple_of(zt * width, width), width)]
        dst = got_own.at[c, rows_at(z * rows, rows), :]
        if d == 0:
            return local(src, dst, own_recv.at[c, z])
        return remote(src, dst, own_send.at[c, d], own_recv.at[c, z], (k, a, zt))

    def hop(c):
        return remote(fc.at[c], prev.at[c], hop_send.at[c], hop_recv.at[c], (k_up, a, z))

    order = [d for d in (1, nlon - 1) if d > 0]
    order = list(dict.fromkeys(order)) + [d for d in range(2, nlon - 1)] + [0]

    @pl.when(k < last)
    def _():
        group = 32

        @pl.loop(0, padded // group)
        def _(i):
            r0 = pl.multiple_of(i * group, group)
            for c in range(fields):
                for s in range(slices):
                    state[c, pl.ds(8 * r0 + s, group, stride=8), :] = slab[
                        c, pl.ds(r0, group), s * lanes : (s + 1) * lanes
                    ]

        lane = lax.broadcasted_iota(jnp.int32, (BLOCK, 8, lanes), 2)
        at_first, at_last = lane == 0, lane == lanes - 1

        def across(v):
            ahead = pltpu.roll(jnp.where(at_first, pltpu.roll(v, 7, 1), v), lanes - 1, 2)
            behind = pltpu.roll(jnp.where(at_last, pltpu.roll(v, 1, 1), v), 1, 2)
            return ahead - behind

        def stage(arg, base, out, keep, mix, gain):
            @pl.loop(0, (padded - HALO) // BLOCK)
            def _(i):
                r0 = 8 + i * BLOCK
                wide = pl.ds(pl.multiple_of(8 * (r0 - 1), 8), 8 * (BLOCK + 2))
                at = pl.ds(pl.multiple_of(8 * r0, 8), 8 * BLOCK)
                h, u, v = [arg[c, wide, :].reshape(BLOCK + 2, 8, lanes) for c in range(3)]
                f2 = frows[at, :].reshape(BLOCK, 8, lanes)
                hm, um, vm = [q[1:-1] for q in (h, u, v)]

                def along(q):
                    return q[2:] - q[:-2]

                dv = v + h * v
                rate_h = across(um + hm * um) + along(dv)
                rate_u = um * across(um) + vm * along(u) + across(hm) - f2 * vm
                rate_v = um * across(vm) + vm * along(v) + along(h) + f2 * um
                for c, (m, rate) in enumerate(((hm, rate_h), (um, rate_u), (vm, rate_v))):
                    if base is None:
                        value = m - gain * rate
                    else:
                        old = base[c, at, :].reshape(BLOCK, 8, lanes)
                        value = keep * old + mix * m - gain * rate
                    out[c, at, :] = value.reshape(8 * BLOCK, lanes)

        half_step = 0.5 * time_step

        @pl.loop(0, STEPS)
        def _(step):
            stage(state, None, mid1, 0.0, 1.0, half_step)
            stage(mid1, state, mid2, 0.75, 0.25, 0.25 * half_step)
            stage(mid2, state, state, 1.0 / 3.0, 2.0 / 3.0, 2.0 / 3.0 * half_step)

        @pl.loop(0, rows // group)
        def _(i):
            r0 = pl.multiple_of(i * group, group)
            for c in range(fields):
                for s in range(slices):
                    fc[c, pl.ds(r0, group), s * lanes : (s + 1) * lanes] = state[
                        c, pl.ds(8 * (r0 + HALO) + s, group, stride=8), :
                    ]

    @pl.when(k == last)
    def _():
        for s in range(nlon):
            block = fc.at[:, :, pl.ds(s * width, width)]
            local(block, block, back_recv.at[s]).wait()
        for d in range(1, nlon):
            backs[d].wait_send()

    for c in range(fields):
        hop(c).start()

    @pl.loop(0, fields)
    def _(c):
        hop(c).wait_recv()
        low, high = filtered(c)
        y_own[c, :, 0:half] = low
        y_own[c, :, half:length] = high
        for d in order:
            home(c, d).start()

    for c in range(fields):
        for s in range(nlon):
            part = pl.ds(s * rows, rows)
            block = got_own.at[c, part, :]
            local(block, block, own_recv.at[c, s]).wait()
            out_ref[c, part, :] = got_own[c, part, :]

    for d in range(1, nlon):
        mains[d].wait_send()
    for up in (True, False):
        for target in range(nlon):
            src, dst, send, recv, lon, lat, crosses = edge(target, up)
            if crosses:
                remote(src, dst, send, recv, (k, lat, jnp.int32(lon))).wait_send()
            else:
                @pl.when(z != lon)
                def _():
                    remote(src, dst, send, recv, (k, lat, jnp.int32(lon))).wait_send()
    for c in range(fields):
        for d in range(nlon):
            if d:
                home(c, d).wait_send()
        hop(c).wait_send()


def solution(mesh):
    nsub, nlat, nlon = mesh.shape["sub"], mesh.shape["lat"], mesh.shape["lon"]

    def shards(launch, backdrop, inverse_variances):
        tile = launch[0]
        fields, lat_rows, width = tile.shape
        length = width * nlon
        half = length // 2
        rows = lat_rows // nlon
        padded = rows + 2 * HALO
        f32, bf16 = jnp.float32, jnp.bfloat16
        dma = pltpu.SemaphoreType.DMA
        any_space = pl.BlockSpec(memory_space=pl.ANY)
        vmem = pl.BlockSpec(memory_space=pltpu.VMEM)
        rows_like = pltpu.VMEM((fields, padded * 8, 128), f32)
        tile_like = pltpu.VMEM((fields, lat_rows, width), f32)
        slab_like = pltpu.VMEM((fields, rows, length), f32)
        out = pl.pallas_call(
            lambda *refs: kernel(nsub, nlat, nlon, *refs),
            name="weighted_defects",
            out_shape=jax.ShapeDtypeStruct(tile.shape, f32),
            in_specs=[any_space, any_space, vmem, any_space,
                      pl.BlockSpec(memory_space=pltpu.SMEM)],
            out_specs=vmem,
            scratch_shapes=[
                pltpu.VMEM((half, length), f32),
                pltpu.VMEM((8, half + 128), f32),
                pltpu.VMEM((8, length), f32),
                pltpu.VMEM((2 * fields, half, half), bf16),
                pltpu.VMEM((2 * fields, half, half), bf16),
                pltpu.VMEM((padded * 8, 128), f32),
                pltpu.VMEM((fields, padded, length), f32),
                slab_like,
                rows_like, rows_like, rows_like,
                slab_like, slab_like, tile_like,
                dma,
                dma((nlon,)), dma((nlon,)), dma((nlon,)),
                dma((nlon,)), dma((nlon,)), dma((nlon,)),
                dma((nlon,)), dma((nlon,)),
                dma((fields, nlon)), dma((fields, nlon)),
                dma((fields,)), dma((fields,)),
            ],
            compiler_params=pltpu.CompilerParams(collective_id=0, has_side_effects=True),
        )(
            tile, backdrop, inverse_variances,
            jnp.asarray(cosine_table(length)), jnp.asarray(doubled_coriolis(lat_rows * nlat)),
        )
        return out[None]

    return jax.shard_map(
        shards,
        mesh=mesh,
        in_specs=(P("sub", None, "lat", "lon"), P(None, "lat", "lon"), P()),
        out_specs=P("sub", None, "lat", "lon"),
        check_vma=False,
    )
```

profile of v0, /device:TPU:1, one launch (start us, length us, event | category | flops | bytes accessed | tf_op | source)
XLA Modules:
  0.0 126.9 jit_solution(4833868446642907995)
XLA Ops:
  0.0 124.2 %weighted_defects.1 = f32[3,512,256]{2,1,0:T(8,128)} custom-call(f32[3,512,256]{2,1,0:T(8,128)} %bitcast.3, f32[3,512,256]{2,1,0:T(8,128)} %refs_1_.1, f32[3,513]{1,0:T(4,128)} %refs_2_.1, f32[512,1024]{1,0:T(8,128)} %constant.4.clone.refs_3_, f32[1024]{0:T(1024)} %constant.5.clone.refs_4_), custom_call_target="tpu_custom_call" | custom-call | tf_op jit(solution)/shard_map/weighted_defects/pallas_call | solution.py:342
  124.2 2.7 %copy.7 = f32[1,3,512,256]{3,2,1,0:T(8,128)} copy(f32[1,3,512,256]{3,2,1,0:T(8,128)} %bitcast.2) | data formatting | bytes 3145728
where the time goes:
time: 127 us
  Pallas kernels  124 us (98%)
  local copies, waits for them, and re-layouts  2.65 us (2%)
    pallas_call x1, Pallas kernels, shards(): pl.pallas_call(lambda *refs: kernel(nsub, nlat, nlon, *refs), name='weigh...  124 us
    unnamed x1, local copies, waits for them, and re-layouts  2.65 us

commit v1 on v0

v1 whole, which is shorter than its diff:
```python
import numpy as np
import jax
import jax.numpy as jnp
from jax import lax
from jax.experimental import pallas as pl
from jax.experimental.pallas import tpu as pltpu
from jax.sharding import PartitionSpec as P

STEPS = 3
PAD = 16
EDGE = 16
SUBLANES = 8
LANES = 128
CHUNK = 8
BLOCK = 4
LAG = 2
MESH = pl.DeviceIdType.MESH

time_step = 0.5
coriolis_peak = 0.4


def cosine_table(length):
    half = length // 2
    wave = np.arange(half)[:, None]
    angle = (wave * np.arange(length)[None, :]) % length * (2.0 * np.pi / length)
    return (np.where(wave == 0, 1.0, 2.0) / length * np.cos(angle)).astype(np.float32)


def doubled_coriolis(total_rows):
    index = np.arange(-PAD, total_rows + PAD)
    line = 2.0 * coriolis_peak * np.sin(2.0 * np.pi * (index + 0.5) / total_rows)
    return np.repeat(line.astype(np.float32)[:, None], LANES, axis=1)


def split_parts(value):
    high = value.astype(jnp.bfloat16)
    return high, (value - high.astype(jnp.float32)).astype(jnp.bfloat16)


def kernel(
    nsub, nlat, nlon, x_hbm, back_hbm, w_ref, table_hbm, f_hbm, out_hbm,
    table, wpad, wave_row, conv_hi, conv_lo, fnat, frows, own, top, bot, corners,
    packed, got_packed, edges, edge_rows, following, slab, y_own, state, mid1, mid2,
    table_sem, f_sem, own_sem, rows_send, rows_recv, corner_send, corner_recv,
    pack_send, pack_recv, next_send, next_recv, in_send, in_recv, out_send, out_recv,
):
    k = lax.axis_index("sub")
    a = lax.axis_index("lat")
    z = lax.axis_index("lon")
    fields, _, span, width = x_hbm.shape
    length = width * nlon
    half = length // 2
    slices = length // LANES
    groups = width // LANES
    ring = groups + 1
    chunks = span // CHUNK
    per = SUBLANES // nlon
    blocks_of_span = span // SUBLANES
    stages = 3 * STEPS
    k_up = lax.rem(k + 1, nsub)
    k_down = lax.rem(k + nsub - 1, nsub)
    a_up = lax.rem(a + 1, nlat)
    a_down = lax.rem(a + nlat - 1, nlat)
    z_up = lax.rem(z + 1, nlon)
    z_down = lax.rem(z + nlon - 1, nlon)
    last = nsub - 1

    barrier = pltpu.get_barrier_semaphore()
    for d in range(1, nlon):
        pl.semaphore_signal(
            barrier, inc=1, device_id=(k, a, lax.rem(z + d, nlon)), device_id_type=MESH
        )
    for d in range(nlon):
        for there in ((k, a_up), (k, a_down), (k_up, a), (k_down, a)):
            pl.semaphore_signal(barrier, inc=1, device_id=there + (jnp.int32(d),), device_id_type=MESH)
    pl.semaphore_wait(barrier, nlon - 1 + 4 * nlon)

    mine = pl.ds(pl.multiple_of(z * width, width), width)

    def local(src, dst, sem):
        return pltpu.make_async_copy(src, dst, sem)

    def remote(src, dst, send, recv, there):
        return pltpu.make_async_remote_copy(
            src_ref=src, dst_ref=dst, send_sem=send, recv_sem=recv,
            device_id=there, device_id_type=MESH,
        )

    def landed(block, sem):
        local(block, block, sem).wait()

    low_rows, high_rows = pl.ds(0, PAD), pl.ds(span - PAD, PAD)
    first_lanes, last_lanes = pl.ds(0, LANES), pl.ds(width - LANES, LANES)

    def row_copies():
        return [
            remote(x_hbm.at[:, SUBLANES - 1, high_rows, :], top, rows_send.at[0], rows_recv.at[0], (k, a_up, z)),
            remote(x_hbm.at[:, 0, low_rows, :], bot, rows_send.at[1], rows_recv.at[1], (k, a_down, z)),
        ]

    def corner_copies():
        copies = []
        for i, (g, rows, lat) in enumerate(((SUBLANES - 1, high_rows, a_up), (0, low_rows, a_down))):
            for j, (cols, lon) in enumerate(((first_lanes, z_down), (last_lanes, z_up))):
                copies.append(remote(
                    x_hbm.at[:, g, rows, cols], corners.at[2 * i + j],
                    corner_send.at[2 * i + j], corner_recv.at[2 * i + j], (k, lat, lon),
                ))
        return copies

    def pack_copies():
        return [
            remote(packed.at[i], got_packed.at[i], pack_send.at[i], pack_recv.at[i], (k, a, lon))
            for i, lon in enumerate((z_down, z_up))
        ]

    def rows_of(c):
        return pl.ds(pl.multiple_of(c * CHUNK, CHUNK), CHUNK)

    def next_copy(c):
        return remote(
            x_hbm.at[:, :, rows_of(c), :], following.at[:, :, rows_of(c), :],
            next_send.at[c], next_recv.at[c], (k_down, a, z),
        )

    def inward(c, d):
        zt = lax.rem(z + d, nlon)
        src = following.at[:, pl.ds(zt * per, per), rows_of(c), :]
        dst = slab.at[:, :, rows_of(c), mine]
        if d == 0:
            return local(src, dst, in_recv.at[c, z])
        return remote(src, dst, in_send.at[c, d], in_recv.at[c, z], (k, a, zt))

    def homeward(c, d):
        zt = lax.rem(z + d, nlon)
        src = y_own.at[:, :, rows_of(c), pl.ds(pl.multiple_of(zt * width, width), width)]
        dst = out_hbm.at[:, pl.ds(z * per, per), rows_of(c), :]
        return remote(src, dst, out_send.at[c, d], out_recv.at[c, z], (k_up, a, zt))

    order = list(range(1, nlon)) + [0]

    def own_copies(src):
        return [local(src.at[c], own.at[c], own_sem.at[c]) for c in range(fields)]

    @pl.when(k < last)
    def _():
        for copy in own_copies(x_hbm):
            copy.start()
        for copy in row_copies() + corner_copies():
            copy.start()

    @pl.when(k == last)
    def _():
        for copy in own_copies(back_hbm):
            copy.start()

    for c in range(chunks):
        next_copy(c).start()
    table_copy = local(table_hbm, table, table_sem)
    f_rows = fnat.shape[0]
    f_copy = local(f_hbm.at[pl.ds(pl.multiple_of(a * (SUBLANES * span), SUBLANES), f_rows), :], fnat, f_sem)
    f_copy.start()
    table_copy.start()

    lane = lax.broadcasted_iota(jnp.int32, (SUBLANES, LANES), 1)

    def strided(r, g):
        return pl.ds(SUBLANES * r + g, SUBLANES, stride=SUBLANES)

    def spread(put, low, main, high):
        for g in range(SUBLANES):
            for b in range((span + 2 * PAD) // SUBLANES):
                r = b * SUBLANES - PAD
                if r < 0:
                    value = low(r + PAD) if g == 0 else main(g - 1, span + r)
                elif r >= span:
                    value = high(r - span) if g == SUBLANES - 1 else main(g + 1, r - span)
                else:
                    value = main(g, r)
                put(strided(b * SUBLANES, g), value)

    @pl.when(k < last)
    def _():
        for copy in own_copies(x_hbm):
            copy.wait()

        @pl.loop(0, fields)
        def _(c):
            for side in range(2):
                cols = pl.ds(0 if side == 0 else width - LANES, LANES)

                @pl.loop(0, SUBLANES)
                def _(g):
                    parts = [own[c, g, pl.ds(SUBLANES * i, SUBLANES), cols] for i in range(blocks_of_span)]
                    step = EDGE
                    while len(parts) > 1:
                        merged = []
                        for i in range(0, len(parts), 2):
                            if side == 0:
                                far = pltpu.roll(parts[i + 1], step, 1)
                                merged.append(jnp.where(lane < step, parts[i], far))
                            else:
                                far = pltpu.roll(parts[i + 1], LANES - step, 1)
                                merged.append(jnp.where(lane >= LANES - step, parts[i], far))
                        parts, step = merged, 2 * step
                    packed[side, c, g] = parts[0]

        for copy in pack_copies():
            copy.start()
        f_copy.wait()
        for g in range(SUBLANES):
            for b in range((span + 2 * PAD) // SUBLANES):
                frows[strided(b * SUBLANES, g), :] = fnat[pl.ds(g * span + b * SUBLANES, SUBLANES), :]
        landed(top, rows_recv.at[0])
        landed(bot, rows_recv.at[1])

        @pl.loop(0, fields)
        def _(c):
            for j in range(groups):
                cols = pl.ds(j * LANES, LANES)

                def put(at, value):
                    state[c, j, at, :] = value

                spread(
                    put,
                    lambda r: top[c, pl.ds(r, SUBLANES), cols],
                    lambda g, r: own[c, g, pl.ds(r, SUBLANES), cols],
                    lambda r: bot[c, pl.ds(r, SUBLANES), cols],
                )

        for i in range(4):
            landed(corners.at[i], corner_recv.at[i])
        for i in range(2):
            landed(got_packed.at[i], pack_recv.at[i])

        def join(right, left):
            return jnp.where(lane < EDGE, right, jnp.where(lane >= LANES - EDGE, left, 0.0))

        @pl.loop(0, fields)
        def _(c):
            for i in range(2):
                for r in range(0, PAD, SUBLANES):
                    at = pl.ds(r, SUBLANES)
                    edge_rows[i, at, :] = join(corners[2 * i, c, at, :], corners[2 * i + 1, c, at, :])

            @pl.loop(0, SUBLANES)
            def _(g):
                right, left = got_packed[0, c, g], got_packed[1, c, g]
                for i in range(blocks_of_span):
                    shift = EDGE * i
                    near = pltpu.roll(right, LANES - shift, 1) if i else right
                    far = pltpu.roll(left, shift, 1) if i else left
                    edges[g, pl.ds(SUBLANES * i, SUBLANES), :] = join(near, far)

            def put(at, value):
                state[c, groups, at, :] = value

            spread(
                put,
                lambda r: edge_rows[0, pl.ds(r, SUBLANES), :],
                lambda g, r: edges[g, pl.ds(r, SUBLANES), :],
                lambda r: edge_rows[1, pl.ds(r, SUBLANES), :],
            )

    @pl.when(k == last)
    def _():
        f_copy.wait()
        for copy in own_copies(back_hbm):
            copy.wait()

    def build_filters():
        wpad[...] = jnp.zeros_like(wpad)
        wpad[0:fields, 0 : half + 1] = w_ref[...]
        table_copy.wait()
        sign = 1.0 - 2.0 * (lax.broadcasted_iota(jnp.int32, (8, length), 1) % 2).astype(jnp.float32)
        wave_row[...] = (
            jnp.dot(
                wpad[:, 0:half], table[...], precision=lax.Precision.HIGHEST,
                preferred_element_type=jnp.float32,
            )
            + wpad[:, half : half + 1] * (sign / length)
        )
        step = 16
        blocks = half // LANES
        for c in range(fields):
            line = 0.5 * wave_row[c : c + 1, :]

            @pl.loop(0, LANES // step)
            def _(i):
                row = i * step + lax.broadcasted_iota(jnp.int32, (step, length), 0)
                turned = jnp.broadcast_to(line, (step, length))
                for bit in range(LANES.bit_length() - 1):
                    far = pltpu.roll(turned, 1 << bit, 1)
                    turned = jnp.where((row >> bit) % 2 == 1, far, turned)
                for q in range(slices):
                    first = turned[:, q * LANES : (q + 1) * LANES]
                    p = (q + blocks) % slices
                    other = turned[:, p * LANES : (p + 1) * LANES]
                    for part, value in enumerate((first + other, first - other)):
                        high, low = split_parts(value)
                        for m in range(blocks):
                            t = (q + m) % slices
                            if t < blocks:
                                at = pl.ds(pl.multiple_of(m * LANES + i * step, step), step)
                                conv_hi[2 * c + part, at, t * LANES : (t + 1) * LANES] = high
                                conv_lo[2 * c + part, at, t * LANES : (t + 1) * LANES] = low

    at_first = lax.broadcasted_iota(jnp.int32, (BLOCK, SUBLANES, LANES), 2) == 0
    at_last = lax.broadcasted_iota(jnp.int32, (BLOCK, SUBLANES, LANES), 2) == LANES - 1

    def across(parts):
        ahead = [pltpu.roll(q, LANES - 1, 2) for q in parts]
        behind = [pltpu.roll(q, 1, 2) for q in parts]
        return [
            jnp.where(at_last, ahead[(j + 1) % ring], ahead[j])
            - jnp.where(at_first, behind[(j - 1) % ring], behind[j])
            for j in range(ring)
        ]

    def stage(arg, base, out, keep, mix, gain, start, blocks):
        @pl.loop(0, blocks)
        def _(i):
            r0 = start + i * BLOCK
            wide = pl.ds(pl.multiple_of(SUBLANES * (r0 - 1), SUBLANES), SUBLANES * (BLOCK + 2))
            at = pl.ds(pl.multiple_of(SUBLANES * r0, SUBLANES), SUBLANES * BLOCK)
            h, u, v = [
                [arg[c, j, wide, :].reshape(BLOCK + 2, SUBLANES, LANES) for j in range(ring)]
                for c in range(3)
            ]
            f2 = frows[at, :].reshape(BLOCK, SUBLANES, LANES)
            hm, um, vm = [[q[1:-1] for q in field] for field in (h, u, v)]

            def along(q):
                return q[2:] - q[:-2]

            flux = across([p + q * p for p, q in zip(um, hm)])
            hx, ux, vx = across(hm), across(um), across(vm)
            for j in range(ring):
                dv = v[j] + h[j] * v[j]
                rate_h = flux[j] + along(dv)
                rate_u = um[j] * ux[j] + vm[j] * along(u[j]) + hx[j] - f2 * vm[j]
                rate_v = um[j] * vx[j] + vm[j] * along(v[j]) + along(h[j]) + f2 * um[j]
                for c, (m, rate) in enumerate(((hm[j], rate_h), (um[j], rate_u), (vm[j], rate_v))):
                    if base is None:
                        value = m - gain * rate
                    else:
                        old = base[c, j, at, :].reshape(BLOCK, SUBLANES, LANES)
                        value = keep * old + mix * m - gain * rate
                    out[c, j, at, :] = value.reshape(SUBLANES * BLOCK, LANES)

    def forecast(c):
        def bounds(t):
            ahead = stages - t
            fill = 2 * ahead + BLOCK - 1
            first = c * CHUNK + ahead
            extra = jnp.where(c == 0, fill - lax.rem(fill, BLOCK), 0)
            return PAD + first - extra, (CHUNK + extra) // BLOCK

        half_step = 0.5 * time_step

        @pl.loop(0, STEPS)
        def _(step):
            stage(state, None, mid1, 0.0, 1.0, half_step, *bounds(3 * step + 1))
            stage(mid1, state, mid2, 0.75, 0.25, 0.25 * half_step, *bounds(3 * step + 2))
            stage(mid2, state, state, 1.0 / 3.0, 2.0 / 3.0, 2.0 / 3.0 * half_step, *bounds(3 * step + 3))

    def filtered(c):
        for s in range(nlon):
            landed(slab.at[:, :, rows_of(c), pl.ds(s * width, width)], in_recv.at[c, s])
        rows = per * CHUNK

        @pl.loop(0, fields)
        def _(field):
            value = slab[field, :, rows_of(c), :].reshape(rows, length)
            left, right = value[:, :half], value[:, half:]
            halves = []
            for part, mix in enumerate((left + right, left - right)):
                high, low = split_parts(mix)
                both = jnp.concatenate([high, low], axis=0)
                twice = jnp.dot(both, conv_hi[2 * field + part], preferred_element_type=jnp.float32)
                rest = jnp.dot(high, conv_lo[2 * field + part], preferred_element_type=jnp.float32)
                halves.append(twice[:rows] + (twice[rows:] + rest))
            y_own[field, :, rows_of(c), 0:half] = (halves[0] + halves[1]).reshape(per, CHUNK, half)
            y_own[field, :, rows_of(c), half:length] = (halves[0] - halves[1]).reshape(per, CHUNK, half)

        for d in order:
            homeward(c, d).start()

    @pl.loop(0, chunks)
    def _(c):
        @pl.when(k < last)
        def _():
            forecast(c)

        landed(following.at[:, :, rows_of(c), :], next_recv.at[c])

        @pl.when(k < last)
        def _():
            @pl.loop(0, fields)
            def _(field):
                for g in range(SUBLANES):
                    at = pl.ds(SUBLANES * (c * CHUNK + PAD) + g, CHUNK, stride=SUBLANES)
                    for j in range(groups):
                        cols = pl.ds(j * LANES, LANES)
                        following[field, g, rows_of(c), cols] = (
                            following[field, g, rows_of(c), cols] - state[field, j, at, :]
                        )

        @pl.when(k == last)
        def _():
            @pl.loop(0, fields)
            def _(field):
                following[field, :, rows_of(c), :] = (
                    following[field, :, rows_of(c), :] - own[field, :, rows_of(c), :]
                )

        for d in order:
            inward(c, d).start()

        @pl.when(c == LAG - 1)
        def _():
            build_filters()

        @pl.when(c >= LAG)
        def _():
            filtered(c - LAG)

    @pl.loop(chunks - LAG, chunks)
    def _(c):
        filtered(c)

    @pl.loop(0, chunks)
    def _(c):
        for s in range(nlon):
            landed(out_hbm.at[:, pl.ds(s * per, per), rows_of(c), :], out_recv.at[c, s])
        next_copy(c).wait_send()
        for d in range(nlon):
            if d:
                inward(c, d).wait_send()
            homeward(c, d).wait_send()

    @pl.when(k < last)
    def _():
        for copy in row_copies() + corner_copies() + pack_copies():
            copy.wait_send()


def solution(mesh):
    nsub, nlat, nlon = mesh.shape["sub"], mesh.shape["lat"], mesh.shape["lon"]

    def shards(launch, backdrop, inverse_variances):
        fields, lat_rows, width = backdrop.shape
        length = width * nlon
        half = length // 2
        span = lat_rows // SUBLANES
        chunks = span // CHUNK
        per = SUBLANES // nlon
        ring = width // LANES + 1
        natural = (fields, SUBLANES, span, width)
        f32, bf16 = jnp.float32, jnp.bfloat16
        dma = pltpu.SemaphoreType.DMA
        any_space = pl.BlockSpec(memory_space=pl.ANY)
        vmem = pl.BlockSpec(memory_space=pltpu.VMEM)
        spread_rows = SUBLANES * (span + 2 * PAD)
        rows_like = pltpu.VMEM((fields, ring, spread_rows, LANES), f32)
        slab_like = pltpu.VMEM((fields, per, span, length), f32)
        out = pl.pallas_call(
            lambda *refs: kernel(nsub, nlat, nlon, *refs),
            name="weighted_defects",
            out_shape=jax.ShapeDtypeStruct(natural, f32),
            in_specs=[any_space, any_space, vmem, any_space, any_space],
            out_specs=any_space,
            scratch_shapes=[
                pltpu.VMEM((half, length), f32),
                pltpu.VMEM((8, half + LANES), f32),
                pltpu.VMEM((8, length), f32),
                pltpu.VMEM((2 * fields, half, half), bf16),
                pltpu.VMEM((2 * fields, half, half), bf16),
                pltpu.VMEM((lat_rows + 2 * PAD, LANES), f32),
                pltpu.VMEM((spread_rows, LANES), f32),
                pltpu.VMEM(natural, f32),
                pltpu.VMEM((fields, PAD, width), f32),
                pltpu.VMEM((fields, PAD, width), f32),
                pltpu.VMEM((4, fields, PAD, LANES), f32),
                pltpu.VMEM((2, fields, SUBLANES, SUBLANES, LANES), f32),
                pltpu.VMEM((2, fields, SUBLANES, SUBLANES, LANES), f32),
                pltpu.VMEM((SUBLANES, span, LANES), f32),
                pltpu.VMEM((2, PAD, LANES), f32),
                pltpu.VMEM(natural, f32),
                slab_like, slab_like,
                rows_like, rows_like, rows_like,
                dma, dma, dma((fields,)),
                dma((2,)), dma((2,)), dma((4,)), dma((4,)), dma((2,)), dma((2,)),
                dma((chunks,)), dma((chunks,)),
                dma((chunks, nlon)), dma((chunks, nlon)), dma((chunks, nlon)), dma((chunks, nlon)),
            ],
            compiler_params=pltpu.CompilerParams(collective_id=0, has_side_effects=True),
        )(
            launch.reshape(natural), backdrop.reshape(natural), inverse_variances,
            jnp.asarray(cosine_table(length)), jnp.asarray(doubled_coriolis(lat_rows * nlat)),
        )
        return out.reshape(launch.shape)

    return jax.shard_map(
        shards,
        mesh=mesh,
        in_specs=(P("sub", None, "lat", "lon"), P(None, "lat", "lon"), P()),
        out_specs=P("sub", None, "lat", "lon"),
        check_vma=False,
    )
```

time: 127 us -> 120 us (0.945)
  Pallas kernels: 124 us -> 117 us
    pallas_call x1, Pallas kernels: 124 us -> 117 us  [shards(): pl.pallas_call(lambda *refs: kernel(nsub, nlat, nlon, *refs), name='weigh...]
where the time goes in v1:
time: 120 us
  Pallas kernels  117 us (98%)
  local copies, waits for them, and re-layouts  2.65 us (2%)
    pallas_call x1, Pallas kernels, shards(): pl.pallas_call(lambda *refs: kernel(nsub, nlat, nlon, *refs), name='weigh...  117 us
    unnamed x1, local copies, waits for them, and re-layouts  2.65 us

profile of v1, /device:TPU:1, one launch (start us, length us, event | category | flops | bytes accessed | tf_op | source)
XLA Modules:
  0.0 119.7 jit_solution(614008459294864231)
XLA Ops:
  0.0 117.0 %weighted_defects.1 = f32[3,8,64,256]{3,2,1,0:T(8,128)} custom-call(f32[3,8,64,256]{3,2,1,0:T(8,128)} %bitcast.4, f32[3,8,64,256]{3,2,1,0:T(8,128)} %bitcast.5, f32[3,513]{1,0:T(4,128)} %refs_2_.1, f32[512,1024]{1,0:T(8,128)} %constant.4.clone.refs_3_, f32[1056,128]{1,0:T(8,128)} %constant.5.clone.refs_4_), custom_call_target="tpu_custom_call" | custom-call | tf_op jit(solution)/shard_map/weighted_defects/pallas_call | solution.py:469
  117.0 2.7 %copy.7 = f32[1,3,512,256]{3,2,1,0:T(8,128)} copy(f32[1,3,512,256]{3,2,1,0:T(8,128)} %bitcast.3) | data formatting | bytes 3145728

commit v2 on v1

--- a/solution.py
+++ b/solution.py
@@ -20,17 +20,27 @@
 coriolis_peak = 0.4
 
 
-def cosine_table(length):
-    half = length // 2
-    wave = np.arange(half)[:, None]
-    angle = (wave * np.arange(length)[None, :]) % length * (2.0 * np.pi / length)
-    return (np.where(wave == 0, 1.0, 2.0) / length * np.cos(angle)).astype(np.float32)
-
-
-def doubled_coriolis(total_rows):
-    index = np.arange(-PAD, total_rows + PAD)
-    line = 2.0 * coriolis_peak * np.sin(2.0 * np.pi * (index + 0.5) / total_rows)
-    return np.repeat(line.astype(np.float32)[:, None], LANES, axis=1)
+def waves(length):
+    half, quarter = length // 2, length // 4
+
+    def basis(points, pairs):
+        n = np.arange(points)
+        columns = []
+        for turn, numbers in pairs:
+            for m in numbers:
+                scale = np.sqrt((1.0 if m in (0, half) else 2.0) / length)
+                columns.append(scale * turn(2.0 * np.pi / length * ((m * n) % length)))
+        return np.stack(columns, axis=1)
+
+    fours = basis(quarter, ((np.cos, range(0, half + 1, 4)), (np.sin, range(4, half, 4))))
+    twos = basis(quarter, ((np.cos, range(2, half, 4)), (np.sin, range(2, half, 4))))
+    odds = basis(half, ((np.cos, range(1, half, 2)), (np.sin, range(1, half, 2))))
+    out = np.stack([
+        np.concatenate([np.concatenate([e, t], axis=1), o], axis=0)
+        for e, t, o in ((fours, twos, odds), (fours.T, twos.T, odds.T))
+    ]).astype(np.float32)
+    high = out.astype(jnp.bfloat16)
+    return np.stack([high, (out - high.astype(np.float32)).astype(jnp.bfloat16)], axis=1)
 
 
 def split_parts(value):
@@ -39,10 +49,10 @@
 
 
 def kernel(
-    nsub, nlat, nlon, x_hbm, back_hbm, w_ref, table_hbm, f_hbm, out_hbm,
-    table, wpad, wave_row, conv_hi, conv_lo, fnat, frows, own, top, bot, corners,
+    nsub, nlat, nlon, x_hbm, back_hbm, w_ref, waves_hbm, out_hbm,
+    waves_ref, wpad, scales, frows, own, top, bot, corners,
     packed, got_packed, edges, edge_rows, following, slab, y_own, state, mid1, mid2,
-    table_sem, f_sem, own_sem, rows_send, rows_recv, corner_send, corner_recv,
+    waves_sem, own_sem, rows_send, rows_recv, corner_send, corner_recv,
     pack_send, pack_recv, next_send, next_recv, in_send, in_recv, out_send, out_recv,
 ):
     k = lax.axis_index("sub")
@@ -51,7 +61,7 @@
     fields, _, span, width = x_hbm.shape
     length = width * nlon
     half = length // 2
-    slices = length // LANES
+    quarter = length // 4
     groups = width // LANES
     ring = groups + 1
     chunks = span // CHUNK
@@ -157,11 +167,8 @@
 
     for c in range(chunks):
         next_copy(c).start()
-    table_copy = local(table_hbm, table, table_sem)
-    f_rows = fnat.shape[0]
-    f_copy = local(f_hbm.at[pl.ds(pl.multiple_of(a * (SUBLANES * span), SUBLANES), f_rows), :], fnat, f_sem)
-    f_copy.start()
-    table_copy.start()
+    waves_copy = local(waves_hbm, waves_ref, waves_sem)
+    waves_copy.start()
 
     lane = lax.broadcasted_iota(jnp.int32, (SUBLANES, LANES), 1)
 
@@ -179,6 +186,14 @@
                 else:
                     value = main(g, r)
                 put(strided(b * SUBLANES, g), value)
+
+    def coriolis_rows():
+        count = SUBLANES * (span + 2 * PAD)
+        total = nlat * SUBLANES * span
+        at = lax.broadcasted_iota(jnp.int32, (count, LANES), 0)
+        row = a * (SUBLANES * span) + lax.rem(at, SUBLANES) * span + at // SUBLANES - PAD
+        row = lax.rem(row + total, total).astype(jnp.float32)
+        frows[...] = (2.0 * coriolis_peak) * jnp.sin((2.0 * np.pi / total) * (row + 0.5))
 
     @pl.when(k < last)
     def _():
@@ -208,10 +223,7 @@
 
         for copy in pack_copies():
             copy.start()
-        f_copy.wait()
-        for g in range(SUBLANES):
-            for b in range((span + 2 * PAD) // SUBLANES):
-                frows[strided(b * SUBLANES, g), :] = fnat[pl.ds(g * span + b * SUBLANES, SUBLANES), :]
+        coriolis_rows()
         landed(top, rows_recv.at[0])
         landed(bot, rows_recv.at[1])
 
@@ -266,56 +278,48 @@
 
     @pl.when(k == last)
     def _():
-        f_copy.wait()
         for copy in own_copies(back_hbm):
             copy.wait()
 
-    def build_filters():
+    def spread_scales():
         wpad[...] = jnp.zeros_like(wpad)
         wpad[0:fields, 0 : half + 1] = w_ref[...]
-        table_copy.wait()
-        sign = 1.0 - 2.0 * (lax.broadcasted_iota(jnp.int32, (8, length), 1) % 2).astype(jnp.float32)
-        wave_row[...] = (
-            jnp.dot(
-                wpad[:, 0:half], table[...], precision=lax.Precision.HIGHEST,
-                preferred_element_type=jnp.float32,
+        depth = wpad.shape[1]
+        parts, rest = [], wpad[...]
+        for _ in range(3):
+            part = rest.astype(jnp.bfloat16).astype(jnp.float32)
+            parts.append(part)
+            rest = rest - part
+        parts = jnp.concatenate(parts + [jnp.zeros_like(rest)], axis=0).astype(jnp.bfloat16)
+        at = lax.broadcasted_iota(jnp.int32, (LANES, length), 1)
+        row = lax.broadcasted_iota(jnp.int32, (LANES, length), 0)
+        eighth = quarter // 2
+        fours = 4 * jnp.where(at <= eighth, at, at - eighth)
+        twos = 4 * lax.rem(at, eighth) + 2
+        odds = 2 * lax.rem(at, quarter) + 1
+        number = jnp.where(at < quarter, fours, jnp.where(at < half, twos, odds))
+        total = jnp.zeros((parts.shape[0], length), jnp.float32)
+        for b in range(depth // LANES):
+            chosen = jnp.where(number == row + b * LANES, 1.0, 0.0).astype(jnp.bfloat16)
+            total += jnp.dot(
+                parts[:, b * LANES : (b + 1) * LANES], chosen, preferred_element_type=jnp.float32
             )
-            + wpad[:, half : half + 1] * (sign / length)
-        )
-        step = 16
-        blocks = half // LANES
+        line = total[0:8] + (total[8:16] + total[16:24])
+        rows = per * CHUNK
         for c in range(fields):
-            line = 0.5 * wave_row[c : c + 1, :]
-
-            @pl.loop(0, LANES // step)
-            def _(i):
-                row = i * step + lax.broadcasted_iota(jnp.int32, (step, length), 0)
-                turned = jnp.broadcast_to(line, (step, length))
-                for bit in range(LANES.bit_length() - 1):
-                    far = pltpu.roll(turned, 1 << bit, 1)
-                    turned = jnp.where((row >> bit) % 2 == 1, far, turned)
-                for q in range(slices):
-                    first = turned[:, q * LANES : (q + 1) * LANES]
-                    p = (q + blocks) % slices
-                    other = turned[:, p * LANES : (p + 1) * LANES]
-                    for part, value in enumerate((first + other, first - other)):
-                        high, low = split_parts(value)
-                        for m in range(blocks):
-                            t = (q + m) % slices
-                            if t < blocks:
-                                at = pl.ds(pl.multiple_of(m * LANES + i * step, step), step)
-                                conv_hi[2 * c + part, at, t * LANES : (t + 1) * LANES] = high
-                                conv_lo[2 * c + part, at, t * LANES : (t + 1) * LANES] = low
+            scales[c * rows : (c + 1) * rows, :] = jnp.broadcast_to(line[c : c + 1, :], (rows, length))
 
     at_first = lax.broadcasted_iota(jnp.int32, (BLOCK, SUBLANES, LANES), 2) == 0
     at_last = lax.broadcasted_iota(jnp.int32, (BLOCK, SUBLANES, LANES), 2) == LANES - 1
 
-    def across(parts):
+    def beside(parts):
         ahead = [pltpu.roll(q, LANES - 1, 2) for q in parts]
         behind = [pltpu.roll(q, 1, 2) for q in parts]
         return [
-            jnp.where(at_last, ahead[(j + 1) % ring], ahead[j])
-            - jnp.where(at_first, behind[(j - 1) % ring], behind[j])
+            (
+                jnp.where(at_last, ahead[(j + 1) % ring], ahead[j]),
+                jnp.where(at_first, behind[(j - 1) % ring], behind[j]),
+            )
             for j in range(ring)
         ]
 
@@ -335,13 +339,13 @@
             def along(q):
                 return q[2:] - q[:-2]
 
-            flux = across([p + q * p for p, q in zip(um, hm)])
-            hx, ux, vx = across(hm), across(um), across(vm)
+            h_by, u_by, v_by = beside(hm), beside(um), beside(vm)
             for j in range(ring):
+                (h1, h0), (u1, u0), (v1, v0) = h_by[j], u_by[j], v_by[j]
                 dv = v[j] + h[j] * v[j]
-                rate_h = flux[j] + along(dv)
-                rate_u = um[j] * ux[j] + vm[j] * along(u[j]) + hx[j] - f2 * vm[j]
-                rate_v = um[j] * vx[j] + vm[j] * along(v[j]) + along(h[j]) + f2 * um[j]
+                rate_h = (u1 + h1 * u1) - (u0 + h0 * u0) + along(dv)
+                rate_u = um[j] * (u1 - u0) + vm[j] * along(u[j]) + (h1 - h0) - f2 * vm[j]
+                rate_v = um[j] * (v1 - v0) + vm[j] * along(v[j]) + along(h[j]) + f2 * um[j]
                 for c, (m, rate) in enumerate(((hm[j], rate_h), (um[j], rate_u), (vm[j], rate_v))):
                     if base is None:
                         value = m - gain * rate
@@ -369,35 +373,69 @@
     def filtered(c):
         for s in range(nlon):
             landed(slab.at[:, :, rows_of(c), pl.ds(s * width, width)], in_recv.at[c, s])
-        rows = per * CHUNK
-
-        @pl.loop(0, fields)
-        def _(field):
-            value = slab[field, :, rows_of(c), :].reshape(rows, length)
-            left, right = value[:, :half], value[:, half:]
-            halves = []
-            for part, mix in enumerate((left + right, left - right)):
-                high, low = split_parts(mix)
-                both = jnp.concatenate([high, low], axis=0)
-                twice = jnp.dot(both, conv_hi[2 * field + part], preferred_element_type=jnp.float32)
-                rest = jnp.dot(high, conv_lo[2 * field + part], preferred_element_type=jnp.float32)
-                halves.append(twice[:rows] + (twice[rows:] + rest))
-            y_own[field, :, rows_of(c), 0:half] = (halves[0] + halves[1]).reshape(per, CHUNK, half)
-            y_own[field, :, rows_of(c), half:length] = (halves[0] - halves[1]).reshape(per, CHUNK, half)
+        rows = fields * per * CHUNK
+
+        def product(value, way, place):
+            high, low = split_parts(value)
+            both = jnp.concatenate([high, low], axis=0)
+            twice = jnp.dot(both, waves_ref[(way, 0) + place], preferred_element_type=jnp.float32)
+            rest = jnp.dot(high, waves_ref[(way, 1) + place], preferred_element_type=jnp.float32)
+            return twice[:rows] + (twice[rows:] + rest)
+
+        value = slab[:, :, rows_of(c), :].reshape(rows, length)
+        left, right = value[:, :half], value[:, half:]
+        even, odd = left + right, left - right
+        places = (
+            (slice(0, quarter), slice(0, quarter)),
+            (slice(0, quarter), slice(quarter, half)),
+            (slice(quarter, quarter + half), slice(0, half)),
+        )
+        inputs = (even[:, :quarter] + even[:, quarter:], even[:, :quarter] - even[:, quarter:], odd)
+        at, outputs = 0, []
+        for place, mix in zip(places, inputs):
+            count = mix.shape[1]
+            coefficients = product(mix, 0, place) * scales[:, at : at + count]
+            outputs.append(product(coefficients, 1, place))
+            at += count
+        fours, twos, odds = outputs
+        for first, even in ((0, fours + twos), (quarter, fours - twos)):
+            part = odds[:, first : first + quarter]
+            for start, result in ((first, even + part), (first + half, even - part)):
+                y_own[:, :, rows_of(c), start : start + quarter] = result.reshape(
+                    fields, per, CHUNK, quarter
+                )
 
         for d in order:
             homeward(c, d).start()
 
-    @pl.loop(0, chunks)
-    def _(c):
-        @pl.when(k < last)
-        def _():
+    def send_defects(c):
+        for d in order:
+            inward(c, d).start()
+
+    @pl.when(k == last)
+    def _():
+        @pl.loop(0, chunks)
+        def _(c):
+            landed(following.at[:, :, rows_of(c), :], next_recv.at[c])
+
+            @pl.loop(0, fields)
+            def _(field):
+                following[field, :, rows_of(c), :] = (
+                    following[field, :, rows_of(c), :] - own[field, :, rows_of(c), :]
+                )
+
+            send_defects(c)
+
+        spread_scales()
+        waves_copy.wait()
+
+    @pl.when(k < last)
+    def _():
+        @pl.loop(0, chunks)
+        def _(c):
             forecast(c)
-
-        landed(following.at[:, :, rows_of(c), :], next_recv.at[c])
-
-        @pl.when(k < last)
-        def _():
+            landed(following.at[:, :, rows_of(c), :], next_recv.at[c])
+
             @pl.loop(0, fields)
             def _(field):
                 for g in range(SUBLANES):
@@ -408,26 +446,18 @@
                             following[field, g, rows_of(c), cols] - state[field, j, at, :]
                         )
 
-        @pl.when(k == last)
-        def _():
-            @pl.loop(0, fields)
-            def _(field):
-                following[field, :, rows_of(c), :] = (
-                    following[field, :, rows_of(c), :] - own[field, :, rows_of(c), :]
-                )
-
-        for d in order:
-            inward(c, d).start()
-
-        @pl.when(c == LAG - 1)
-        def _():
-            build_filters()
-
-        @pl.when(c >= LAG)
-        def _():
-            filtered(c - LAG)
-
-    @pl.loop(chunks - LAG, chunks)
+            send_defects(c)
+
+            @pl.when(c == 0)
+            def _():
+                spread_scales()
+                waves_copy.wait()
+
+            @pl.when(c >= LAG)
+            def _():
+                filtered(c - LAG)
+
+    @pl.loop(jnp.where(k == last, 0, chunks - LAG), chunks)
     def _(c):
         filtered(c)
 
@@ -470,15 +500,12 @@
             lambda *refs: kernel(nsub, nlat, nlon, *refs),
             name="weighted_defects",
             out_shape=jax.ShapeDtypeStruct(natural, f32),
-            in_specs=[any_space, any_space, vmem, any_space, any_space],
+            in_specs=[any_space, any_space, vmem, any_space],
             out_specs=any_space,
             scratch_shapes=[
-                pltpu.VMEM((half, length), f32),
+                pltpu.VMEM((2, 2, half + half // 2, half), bf16),
                 pltpu.VMEM((8, half + LANES), f32),
-                pltpu.VMEM((8, length), f32),
-                pltpu.VMEM((2 * fields, half, half), bf16),
-                pltpu.VMEM((2 * fields, half, half), bf16),
-                pltpu.VMEM((lat_rows + 2 * PAD, LANES), f32),
+                pltpu.VMEM((fields * per * CHUNK, length), f32),
                 pltpu.VMEM((spread_rows, LANES), f32),
                 pltpu.VMEM(natural, f32),
                 pltpu.VMEM((fields, PAD, width), f32),
@@ -491,7 +518,7 @@
                 pltpu.VMEM(natural, f32),
                 slab_like, slab_like,
                 rows_like, rows_like, rows_like,
-                dma, dma, dma((fields,)),
+                dma, dma((fields,)),
                 dma((2,)), dma((2,)), dma((4,)), dma((4,)), dma((2,)), dma((2,)),
                 dma((chunks,)), dma((chunks,)),
                 dma((chunks, nlon)), dma((chunks, nlon)), dma((chunks, nlon)), dma((chunks, nlon)),
@@ -499,7 +526,7 @@
             compiler_params=pltpu.CompilerParams(collective_id=0, has_side_effects=True),
         )(
             launch.reshape(natural), backdrop.reshape(natural), inverse_variances,
-            jnp.asarray(cosine_table(length)), jnp.asarray(doubled_coriolis(lat_rows * nlat)),
+            jnp.asarray(waves(length)),
         )
         return out.reshape(launch.shape)
 

time: 120 us -> 105 us (0.88)
  Pallas kernels: 117 us -> 102 us
    pallas_call x1, Pallas kernels: 117 us -> 102 us  [shards(): pl.pallas_call(lambda *refs: kernel(nsub, nlat, nlon, *refs), name='weigh...]
where the time goes in v2:
time: 105 us
  Pallas kernels  102 us (97%)
  local copies, waits for them, and re-layouts  2.65 us (3%)
    pallas_call x1, Pallas kernels, shards(): pl.pallas_call(lambda *refs: kernel(nsub, nlat, nlon, *refs), name='weigh...  102 us
    unnamed x1, local copies, waits for them, and re-layouts  2.65 us

profile of v2, /device:TPU:1, one launch (start us, length us, event | category | flops | bytes accessed | tf_op | source)
XLA Modules:
  0.0 104.9 jit_solution(6565898872758876754)
XLA Ops:
  0.0 102.2 %weighted_defects.1 = f32[3,8,64,256]{3,2,1,0:T(8,128)} custom-call(f32[3,8,64,256]{3,2,1,0:T(8,128)} %bitcast.4, f32[3,8,64,256]{3,2,1,0:T(8,128)} %bitcast.5, f32[3,513]{1,0:T(4,128)} %refs_2_.1, bf16[2,2,768,512]{3,2,1,0:T(8,128)(2,1)} %constant.2.clone.refs_3_), custom_call_target="tpu_custom_call" | custom-call | tf_op jit(solution)/shard_map/weighted_defects/pallas_call | solution.py:499
  102.2 2.7 %copy.6 = f32[1,3,512,256]{3,2,1,0:T(8,128)} copy(f32[1,3,512,256]{3,2,1,0:T(8,128)} %bitcast.3) | data formatting | bytes 3145728

commit v3 on v2

--- a/solution.py
+++ b/solution.py
@@ -13,7 +13,7 @@
 LANES = 128
 CHUNK = 8
 BLOCK = 4
-LAG = 2
+LAG = 3
 MESH = pl.DeviceIdType.MESH
 
 time_step = 0.5
@@ -51,7 +51,7 @@
 def kernel(
     nsub, nlat, nlon, x_hbm, back_hbm, w_ref, waves_hbm, out_hbm,
     waves_ref, wpad, scales, frows, own, top, bot, corners,
-    packed, got_packed, edges, edge_rows, following, slab, y_own, state, mid1, mid2,
+    corner_packs, packed, got_packed, following, slab, y_own, state, mid1, mid2,
     waves_sem, own_sem, rows_send, rows_recv, corner_send, corner_recv,
     pack_send, pack_recv, next_send, next_recv, in_send, in_recv, out_send, out_recv,
 ):
@@ -66,7 +66,6 @@
     ring = groups + 1
     chunks = span // CHUNK
     per = SUBLANES // nlon
-    blocks_of_span = span // SUBLANES
     stages = 3 * STEPS
     k_up = lax.rem(k + 1, nsub)
     k_down = lax.rem(k + nsub - 1, nsub)
@@ -84,7 +83,6 @@
     for d in range(nlon):
         for there in ((k, a_up), (k, a_down), (k_up, a), (k_down, a)):
             pl.semaphore_signal(barrier, inc=1, device_id=there + (jnp.int32(d),), device_id_type=MESH)
-    pl.semaphore_wait(barrier, nlon - 1 + 4 * nlon)
 
     mine = pl.ds(pl.multiple_of(z * width, width), width)
 
@@ -110,18 +108,28 @@
         ]
 
     def corner_copies():
-        copies = []
-        for i, (g, rows, lat) in enumerate(((SUBLANES - 1, high_rows, a_up), (0, low_rows, a_down))):
-            for j, (cols, lon) in enumerate(((first_lanes, z_down), (last_lanes, z_up))):
-                copies.append(remote(
-                    x_hbm.at[:, g, rows, cols], corners.at[2 * i + j],
-                    corner_send.at[2 * i + j], corner_recv.at[2 * i + j], (k, lat, lon),
-                ))
-        return copies
-
-    def pack_copies():
         return [
-            remote(packed.at[i], got_packed.at[i], pack_send.at[i], pack_recv.at[i], (k, a, lon))
+            remote(
+                corner_packs.at[2 * i + j], corners.at[2 * i + j],
+                corner_send.at[2 * i + j], corner_recv.at[2 * i + j], (k, lat, lon),
+            )
+            for i, lat in enumerate((a_up, a_down)) for j, lon in enumerate((z_down, z_up))
+        ]
+
+    blocks_of_span = span // SUBLANES
+    early = blocks_of_span // 2 + 1
+    turn = PAD // SUBLANES
+
+    def place_of(i):
+        return (i + turn) % blocks_of_span
+
+    def pack_copies(part):
+        at = pl.ds(0, early) if part == 0 else pl.ds(early, blocks_of_span - early)
+        return [
+            remote(
+                packed.at[i, :, at], got_packed.at[i, :, at],
+                pack_send.at[part, i], pack_recv.at[part, i], (k, a, lon),
+            )
             for i, lon in enumerate((z_down, z_up))
         ]
 
@@ -157,16 +165,12 @@
     def _():
         for copy in own_copies(x_hbm):
             copy.start()
-        for copy in row_copies() + corner_copies():
-            copy.start()
 
     @pl.when(k == last)
     def _():
         for copy in own_copies(back_hbm):
             copy.start()
 
-    for c in range(chunks):
-        next_copy(c).start()
     waves_copy = local(waves_hbm, waves_ref, waves_sem)
     waves_copy.start()
 
@@ -195,6 +199,33 @@
         row = lax.rem(row + total, total).astype(jnp.float32)
         frows[...] = (2.0 * coriolis_peak) * jnp.sin((2.0 * np.pi / total) * (row + 0.5))
 
+    def merge(parts, side):
+        step = EDGE
+        while len(parts) > 1:
+            merged = []
+            for i in range(0, len(parts) - 1, 2):
+                if side == 0:
+                    far = pltpu.roll(parts[i + 1], step, 1)
+                    merged.append(jnp.where(lanes_of(far) < step, parts[i], far))
+                else:
+                    far = pltpu.roll(parts[i + 1], LANES - step, 1)
+                    merged.append(jnp.where(lanes_of(far) >= LANES - step, parts[i], far))
+            if len(parts) % 2:
+                merged.append(parts[-1])
+            parts, step = merged, 2 * step
+        return parts[0]
+
+    def lanes_of(value):
+        return lax.broadcasted_iota(jnp.int32, value.shape, len(value.shape) - 1)
+
+    def join(right, left, slot):
+        shift = EDGE * slot
+        near = pltpu.roll(right, LANES - shift, 1) if slot else right
+        far = pltpu.roll(left, shift, 1) if slot else left
+        return jnp.where(lane < EDGE, near, jnp.where(lane >= LANES - EDGE, far, 0.0))
+
+    ends = ((SUBLANES - 1, span - PAD), (0, 0))
+
     @pl.when(k < last)
     def _():
         for copy in own_copies(x_hbm):
@@ -204,26 +235,66 @@
         def _(c):
             for side in range(2):
                 cols = pl.ds(0 if side == 0 else width - LANES, LANES)
-
-                @pl.loop(0, SUBLANES)
-                def _(g):
-                    parts = [own[c, g, pl.ds(SUBLANES * i, SUBLANES), cols] for i in range(blocks_of_span)]
-                    step = EDGE
-                    while len(parts) > 1:
-                        merged = []
-                        for i in range(0, len(parts), 2):
-                            if side == 0:
-                                far = pltpu.roll(parts[i + 1], step, 1)
-                                merged.append(jnp.where(lane < step, parts[i], far))
-                            else:
-                                far = pltpu.roll(parts[i + 1], LANES - step, 1)
-                                merged.append(jnp.where(lane >= LANES - step, parts[i], far))
-                        parts, step = merged, 2 * step
-                    packed[side, c, g] = parts[0]
-
-        for copy in pack_copies():
+                whole = merge([own[c, g, :, cols] for g in range(SUBLANES)], side)
+                for i in range(blocks_of_span):
+                    packed[side, c, place_of(i)] = whole[SUBLANES * i : SUBLANES * (i + 1)]
+
+        for i, (g, first) in enumerate(ends):
+            for side in range(2):
+                cols = pl.ds(0 if side == 0 else width - LANES, LANES)
+                corner_packs[2 * i + side] = merge(
+                    [
+                        own[c, g, pl.ds(first + SUBLANES * b, SUBLANES), cols]
+                        for c in range(fields) for b in range(turn)
+                    ],
+                    side,
+                )
+        coriolis_rows()
+
+    pl.semaphore_wait(barrier, nlon - 1 + 4 * nlon)
+
+    @pl.when(k < last)
+    def _():
+        for copy in pack_copies(0) + row_copies() + corner_copies() + pack_copies(1):
             copy.start()
-        coriolis_rows()
+
+    for c in range(chunks):
+        next_copy(c).start()
+
+    def edge_blocks(numbers, corner):
+        @pl.loop(0, fields)
+        def _(c):
+            def put(r, g, value):
+                state[c, groups, strided(r + PAD, g), :] = value
+
+            for i in numbers:
+                right, left = got_packed[0, c, place_of(i)], got_packed[1, c, place_of(i)]
+                for g in range(SUBLANES):
+                    value = join(right, left, g)
+                    r = SUBLANES * i
+                    put(r, g, value)
+                    if r >= span - PAD and g < SUBLANES - 1:
+                        put(r - span, g + 1, value)
+                    if r < PAD and g > 0:
+                        put(r + span, g - 1, value)
+
+        for c in range(fields):
+            for b in range(turn):
+                value = join(corners[2 * corner], corners[2 * corner + 1], c * turn + b)
+                g, r = ((0, -PAD), (SUBLANES - 1, span))[corner]
+                state[c, groups, strided(r + SUBLANES * b + PAD, g), :] = value
+
+    early_blocks = [i for i in range(blocks_of_span) if place_of(i) < early]
+    late_blocks = [i for i in range(blocks_of_span) if place_of(i) >= early]
+
+    def late_edges():
+        for i in range(2):
+            landed(got_packed.at[i, :, pl.ds(early, blocks_of_span - early)], pack_recv.at[1, i])
+            landed(corners.at[2 + i], corner_recv.at[2 + i])
+        edge_blocks(late_blocks, 1)
+
+    @pl.when(k < last)
+    def _():
         landed(top, rows_recv.at[0])
         landed(bot, rows_recv.at[1])
 
@@ -242,39 +313,10 @@
                     lambda r: bot[c, pl.ds(r, SUBLANES), cols],
                 )
 
-        for i in range(4):
+        for i in range(2):
+            landed(got_packed.at[i, :, pl.ds(0, early)], pack_recv.at[0, i])
             landed(corners.at[i], corner_recv.at[i])
-        for i in range(2):
-            landed(got_packed.at[i], pack_recv.at[i])
-
-        def join(right, left):
-            return jnp.where(lane < EDGE, right, jnp.where(lane >= LANES - EDGE, left, 0.0))
-
-        @pl.loop(0, fields)
-        def _(c):
-            for i in range(2):
-                for r in range(0, PAD, SUBLANES):
-                    at = pl.ds(r, SUBLANES)
-                    edge_rows[i, at, :] = join(corners[2 * i, c, at, :], corners[2 * i + 1, c, at, :])
-
-            @pl.loop(0, SUBLANES)
-            def _(g):
-                right, left = got_packed[0, c, g], got_packed[1, c, g]
-                for i in range(blocks_of_span):
-                    shift = EDGE * i
-                    near = pltpu.roll(right, LANES - shift, 1) if i else right
-                    far = pltpu.roll(left, shift, 1) if i else left
-                    edges[g, pl.ds(SUBLANES * i, SUBLANES), :] = join(near, far)
-
-            def put(at, value):
-                state[c, groups, at, :] = value
-
-            spread(
-                put,
-                lambda r: edge_rows[0, pl.ds(r, SUBLANES), :],
-                lambda g, r: edges[g, pl.ds(r, SUBLANES), :],
-                lambda r: edge_rows[1, pl.ds(r, SUBLANES), :],
-            )
+        edge_blocks(early_blocks, 0)
 
     @pl.when(k == last)
     def _():
@@ -450,6 +492,7 @@
 
             @pl.when(c == 0)
             def _():
+                late_edges()
                 spread_scales()
                 waves_copy.wait()
 
@@ -473,7 +516,7 @@
 
     @pl.when(k < last)
     def _():
-        for copy in row_copies() + corner_copies() + pack_copies():
+        for copy in row_copies() + corner_copies() + pack_copies(0) + pack_copies(1):
             copy.wait_send()
 
 
@@ -494,6 +537,8 @@
         any_space = pl.BlockSpec(memory_space=pl.ANY)
         vmem = pl.BlockSpec(memory_space=pltpu.VMEM)
         spread_rows = SUBLANES * (span + 2 * PAD)
+        corner_like = pltpu.VMEM((4, SUBLANES, LANES), f32)
+        pack_like = pltpu.VMEM((2, fields, span // SUBLANES, SUBLANES, LANES), f32)
         rows_like = pltpu.VMEM((fields, ring, spread_rows, LANES), f32)
         slab_like = pltpu.VMEM((fields, per, span, length), f32)
         out = pl.pallas_call(
@@ -510,16 +555,12 @@
                 pltpu.VMEM(natural, f32),
                 pltpu.VMEM((fields, PAD, width), f32),
                 pltpu.VMEM((fields, PAD, width), f32),
-                pltpu.VMEM((4, fields, PAD, LANES), f32),
-                pltpu.VMEM((2, fields, SUBLANES, SUBLANES, LANES), f32),
-                pltpu.VMEM((2, fields, SUBLANES, SUBLANES, LANES), f32),
-                pltpu.VMEM((SUBLANES, span, LANES), f32),
-                pltpu.VMEM((2, PAD, LANES), f32),
+                corner_like, corner_like, pack_like, pack_like,
                 pltpu.VMEM(natural, f32),
                 slab_like, slab_like,
                 rows_like, rows_like, rows_like,
                 dma, dma((fields,)),
-                dma((2,)), dma((2,)), dma((4,)), dma((4,)), dma((2,)), dma((2,)),
+                dma((2,)), dma((2,)), dma((4,)), dma((4,)), dma((2, 2)), dma((2, 2)),
                 dma((chunks,)), dma((chunks,)),
                 dma((chunks, nlon)), dma((chunks, nlon)), dma((chunks, nlon)), dma((chunks, nlon)),
             ],

time: 105 us -> 93 us (0.89)
  Pallas kernels: 102 us -> 90.1 us
    pallas_call x1, Pallas kernels: 102 us -> 90.1 us  [shards(): pl.pallas_call(lambda *refs: kernel(nsub, nlat, nlon, *refs), name='weigh...]
where the time goes in v3:
time: 93 us; the launch traced here: 92.7 us
  Pallas kernels  90.1 us (97%)
  local copies, waits for them, and re-layouts  2.65 us (3%)
    pallas_call x1, Pallas kernels, shards(): pl.pallas_call(lambda *refs: kernel(nsub, nlat, nlon, *refs), name='weigh...  90.1 us
    unnamed x1, local copies, waits for them, and re-layouts  2.65 us

profile of v3, /device:TPU:1, one launch (start us, length us, event | category | flops | bytes accessed | tf_op | source)
XLA Modules:
  0.0 92.7 jit_solution(8473802374952830075)
XLA Ops:
  0.0 90.1 %weighted_defects.1 = f32[3,8,64,256]{3,2,1,0:T(8,128)} custom-call(f32[3,8,64,256]{3,2,1,0:T(8,128)} %bitcast.4, f32[3,8,64,256]{3,2,1,0:T(8,128)} %bitcast.5, f32[3,513]{1,0:T(4,128)} %refs_2_.1, bf16[2,2,768,512]{3,2,1,0:T(8,128)(2,1)} %constant.2.clone.refs_3_), custom_call_target="tpu_custom_call" | custom-call | tf_op jit(solution)/shard_map/weighted_defects/pallas_call | solution.py:544
  90.1 2.7 %copy.6 = f32[1,3,512,256]{3,2,1,0:T(8,128)} copy(f32[1,3,512,256]{3,2,1,0:T(8,128)} %bitcast.3) | data formatting | bytes 3145728

commit v4 on v3

--- a/solution.py
+++ b/solution.py
@@ -14,6 +14,7 @@
 CHUNK = 8
 BLOCK = 4
 LAG = 3
+VMEM_LIMIT = 52 * 2**20
 MESH = pl.DeviceIdType.MESH
 
 time_step = 0.5
@@ -51,9 +52,9 @@
 def kernel(
     nsub, nlat, nlon, x_hbm, back_hbm, w_ref, waves_hbm, out_hbm,
     waves_ref, wpad, scales, frows, own, top, bot, corners,
-    corner_packs, packed, got_packed, following, slab, y_own, state, mid1, mid2,
+    corner_packs, packed, got_packed, following, relayed, slab, y_own, state, mid1, mid2,
     waves_sem, own_sem, rows_send, rows_recv, corner_send, corner_recv,
-    pack_send, pack_recv, next_send, next_recv, in_send, in_recv, out_send, out_recv,
+    pack_send, pack_recv, next_send, next_recv, relay_send, relay_recv, in_send, in_recv, out_send, out_recv,
 ):
     k = lax.axis_index("sub")
     a = lax.axis_index("lat")
@@ -74,6 +75,7 @@
     z_up = lax.rem(z + 1, nlon)
     z_down = lax.rem(z + nlon - 1, nlon)
     last = nsub - 1
+    giver, taker = (last - 2, last - 1) if nsub > 2 else (-1, -1)
 
     barrier = pltpu.get_barrier_semaphore()
     for d in range(1, nlon):
@@ -142,19 +144,29 @@
             next_send.at[c], next_recv.at[c], (k_down, a, z),
         )
 
-    def inward(c, d):
+    def inward(c, d, block=None):
         zt = lax.rem(z + d, nlon)
-        src = following.at[:, pl.ds(zt * per, per), rows_of(c), :]
+        if block is None:
+            block = following.at[:, :, rows_of(c), :]
+        src = block.at[:, pl.ds(zt * per, per)]
         dst = slab.at[:, :, rows_of(c), mine]
         if d == 0:
             return local(src, dst, in_recv.at[c, z])
         return remote(src, dst, in_send.at[c, d], in_recv.at[c, z], (k, a, zt))
 
-    def homeward(c, d):
+    def relay():
+        return remote(following.at[:, :, rows_of(chunks - 1), :], relayed, relay_send, relay_recv, (k_up, a, z))
+
+    def homeward(c, d, target=None):
         zt = lax.rem(z + d, nlon)
+        home = c if target is None else target
         src = y_own.at[:, :, rows_of(c), pl.ds(pl.multiple_of(zt * width, width), width)]
-        dst = out_hbm.at[:, pl.ds(z * per, per), rows_of(c), :]
-        return remote(src, dst, out_send.at[c, d], out_recv.at[c, z], (k_up, a, zt))
+        dst = out_hbm.at[:, pl.ds(z * per, per), rows_of(home), :]
+        if target is not None and d == 0:
+            return local(src, dst, out_recv.at[home, z])
+        return remote(
+            src, dst, out_send.at[c, d], out_recv.at[home, z], (k_up if target is None else k, a, zt)
+        )
 
     order = list(range(1, nlon)) + [0]
 
@@ -192,12 +204,16 @@
                 put(strided(b * SUBLANES, g), value)
 
     def coriolis_rows():
-        count = SUBLANES * (span + 2 * PAD)
         total = nlat * SUBLANES * span
-        at = lax.broadcasted_iota(jnp.int32, (count, LANES), 0)
-        row = a * (SUBLANES * span) + lax.rem(at, SUBLANES) * span + at // SUBLANES - PAD
-        row = lax.rem(row + total, total).astype(jnp.float32)
-        frows[...] = (2.0 * coriolis_peak) * jnp.sin((2.0 * np.pi / total) * (row + 0.5))
+        group = lax.broadcasted_iota(jnp.int32, (SUBLANES, LANES), 0)
+        for first in range(0, span + 2 * PAD, LANES):
+            row = a * (SUBLANES * span) + group * span + lane + (first - PAD)
+            row = lax.rem(row + total, total).astype(jnp.float32)
+            line = (2.0 * coriolis_peak) * jnp.sin((2.0 * np.pi / total) * (row + 0.5))
+            for r in range(first, min(first + LANES, span + 2 * PAD)):
+                frows[SUBLANES * r : SUBLANES * (r + 1), :] = jnp.broadcast_to(
+                    line[:, r - first : r - first + 1], (SUBLANES, LANES)
+                )
 
     def merge(parts, side):
         step = EDGE
@@ -249,7 +265,6 @@
                     ],
                     side,
                 )
-        coriolis_rows()
 
     pl.semaphore_wait(barrier, nlon - 1 + 4 * nlon)
 
@@ -295,6 +310,7 @@
 
     @pl.when(k < last)
     def _():
+        coriolis_rows()
         landed(top, rows_recv.at[0])
         landed(bot, rows_recv.at[1])
 
@@ -447,8 +463,15 @@
                     fields, per, CHUNK, quarter
                 )
 
-        for d in order:
-            homeward(c, d).start()
+        @pl.when(c < chunks)
+        def _():
+            for d in order:
+                homeward(c, d).start()
+
+        @pl.when(c == chunks)
+        def _():
+            for d in order:
+                homeward(chunks, d, chunks - 1).start()
 
     def send_defects(c):
         for d in order:
@@ -488,7 +511,15 @@
                             following[field, g, rows_of(c), cols] - state[field, j, at, :]
                         )
 
-            send_defects(c)
+            passes = (k == giver) & (c == chunks - 1)
+
+            @pl.when(passes)
+            def _():
+                relay().start()
+
+            @pl.when(jnp.logical_not(passes))
+            def _():
+                send_defects(c)
 
             @pl.when(c == 0)
             def _():
@@ -500,19 +531,37 @@
             def _():
                 filtered(c - LAG)
 
-    @pl.loop(jnp.where(k == last, 0, chunks - LAG), chunks)
+    handled = chunks + (k == taker).astype(jnp.int32) - (k == giver).astype(jnp.int32)
+
+    @pl.loop(jnp.where(k == last, 0, chunks - LAG), handled)
     def _(c):
         filtered(c)
+
+        @pl.when((k == taker) & (c == chunks - LAG))
+        def _():
+            landed(relayed, relay_recv)
+            for d in order:
+                inward(chunks, d, relayed).start()
 
     @pl.loop(0, chunks)
     def _(c):
         for s in range(nlon):
             landed(out_hbm.at[:, pl.ds(s * per, per), rows_of(c), :], out_recv.at[c, s])
         next_copy(c).wait_send()
-        for d in range(nlon):
-            if d:
-                inward(c, d).wait_send()
-            homeward(c, d).wait_send()
+
+    @pl.loop(0, handled)
+    def _(c):
+        for d in range(1, nlon):
+            inward(c, d, relayed).wait_send()
+            homeward(c, d, 0).wait_send()
+
+        @pl.when(c < chunks)
+        def _():
+            homeward(c, 0).wait_send()
+
+    @pl.when(k == giver)
+    def _():
+        relay().wait_send()
 
     @pl.when(k < last)
     def _():
@@ -540,7 +589,7 @@
         corner_like = pltpu.VMEM((4, SUBLANES, LANES), f32)
         pack_like = pltpu.VMEM((2, fields, span // SUBLANES, SUBLANES, LANES), f32)
         rows_like = pltpu.VMEM((fields, ring, spread_rows, LANES), f32)
-        slab_like = pltpu.VMEM((fields, per, span, length), f32)
+        slab_like = pltpu.VMEM((fields, per, span + CHUNK, length), f32)
         out = pl.pallas_call(
             lambda *refs: kernel(nsub, nlat, nlon, *refs),
             name="weighted_defects",
@@ -557,14 +606,16 @@
                 pltpu.VMEM((fields, PAD, width), f32),
                 corner_like, corner_like, pack_like, pack_like,
                 pltpu.VMEM(natural, f32),
+                pltpu.VMEM((fields, SUBLANES, CHUNK, width), f32),
                 slab_like, slab_like,
                 rows_like, rows_like, rows_like,
                 dma, dma((fields,)),
                 dma((2,)), dma((2,)), dma((4,)), dma((4,)), dma((2, 2)), dma((2, 2)),
-                dma((chunks,)), dma((chunks,)),
-                dma((chunks, nlon)), dma((chunks, nlon)), dma((chunks, nlon)), dma((chunks, nlon)),
+                dma((chunks,)), dma((chunks,)), dma, dma,
+                dma((chunks + 1, nlon)), dma((chunks + 1, nlon)),
+                dma((chunks + 1, nlon)), dma((chunks, nlon)),
             ],
-            compiler_params=pltpu.CompilerParams(collective_id=0, has_side_effects=True),
+            compiler_params=pltpu.CompilerParams(collective_id=0, has_side_effects=True, vmem_limit_bytes=VMEM_LIMIT),
         )(
             launch.reshape(natural), backdrop.reshape(natural), inverse_variances,
             jnp.asarray(waves(length)),

time: 93 us -> 87.5 us (0.941)
  Pallas kernels: 90.1 us -> 84.5 us
    pallas_call x1, Pallas kernels: 90.1 us -> 84.5 us  [shards(): pl.pallas_call(lambda *refs: kernel(nsub, nlat, nlon, *refs), name='weigh...]
    unnamed x1 -> x3, local copies, waits for them, and re-layouts: 2.65 us -> 1.85 us
where the time goes in v4:
time: 87.5 us; the launch traced here: 86.4 us
  Pallas kernels  84.5 us (97%)
  local copies, waits for them, and re-layouts  1.85 us (2%)
    pallas_call x1, Pallas kernels, shards(): pl.pallas_call(lambda *refs: kernel(nsub, nlat, nlon, *refs), name='weigh...  84.5 us
    unnamed x3, local copies, waits for them, and re-layouts  1.85 us

profile of v4, /device:TPU:1, one launch (start us, length us, event | category | flops | bytes accessed | tf_op | source)
XLA Modules:
  0.0 86.4 jit_solution(15268902785087334023)
XLA Ops:
  0.0 0.0 copy-start
  0.0 0.7 copy-done
  0.7 84.5 %weighted_defects.1 = f32[3,8,64,256]{3,2,1,0:T(8,128)S(1)} custom-call(f32[3,8,64,256]{3,2,1,0:T(8,128)} %bitcast.4, f32[3,8,64,256]{3,2,1,0:T(8,128)} %bitcast.5, f32[3,513]{1,0:T(4,128)S(1)} %copy-done, bf16[2,2,768,512]{3,2,1,0:T(8,128)(2,1)} %constant.2.clone.refs_3_), custom_call_target="tpu_custom_call" | custom-call | tf_op jit(solution)/shard_map/weighted_defects/pallas_call | solution.py:593
  85.3 1.1 %copy.6 = f32[1,3,512,256]{3,2,1,0:T(8,128)} copy(f32[1,3,512,256]{3,2,1,0:T(8,128)S(1)} %bitcast.3) | data formatting | bytes 3145728
Async XLA Ops:
  0.0 0.7 copy-start

commit v5 on v4

--- a/solution.py
+++ b/solution.py
@@ -14,6 +14,7 @@
 CHUNK = 8
 BLOCK = 4
 LAG = 3
+EXTRA = 5
 VMEM_LIMIT = 52 * 2**20
 MESH = pl.DeviceIdType.MESH
 
@@ -52,8 +53,8 @@
 def kernel(
     nsub, nlat, nlon, x_hbm, back_hbm, w_ref, waves_hbm, out_hbm,
     waves_ref, wpad, scales, frows, own, top, bot, corners,
-    corner_packs, packed, got_packed, following, relayed, slab, y_own, state, mid1, mid2,
-    waves_sem, own_sem, rows_send, rows_recv, corner_send, corner_recv,
+    corner_packs, packed, got_packed, following, extra, slab, y_own, state, mid1, mid2,
+    waves_sem, own_sem, extra_sem, rows_send, rows_recv, corner_send, corner_recv,
     pack_send, pack_recv, next_send, next_recv, relay_send, relay_recv, in_send, in_recv, out_send, out_recv,
 ):
     k = lax.axis_index("sub")
@@ -76,6 +77,11 @@
     z_down = lax.rem(z + nlon - 1, nlon)
     last = nsub - 1
     giver, taker = (last - 2, last - 1) if nsub > 2 else (-1, -1)
+    kept = chunks - EXTRA
+    is_giver, is_taker = (k == giver).astype(jnp.int32), (k == taker).astype(jnp.int32)
+    is_first, is_last = (k == 0).astype(jnp.int32), (k == last).astype(jnp.int32)
+    n_own = chunks - EXTRA * (is_giver + is_last)
+    n_extra = EXTRA * (is_taker + is_first)
 
     barrier = pltpu.get_barrier_semaphore()
     for d in range(1, nlon):
@@ -144,28 +150,30 @@
             next_send.at[c], next_recv.at[c], (k_down, a, z),
         )
 
-    def inward(c, d, block=None):
+    def inward(c, d, extras=False):
         zt = lax.rem(z + d, nlon)
-        if block is None:
-            block = following.at[:, :, rows_of(c), :]
+        block = extra.at[:, :, rows_of(c - chunks), :] if extras else following.at[:, :, rows_of(c), :]
         src = block.at[:, pl.ds(zt * per, per)]
         dst = slab.at[:, :, rows_of(c), mine]
         if d == 0:
             return local(src, dst, in_recv.at[c, z])
         return remote(src, dst, in_send.at[c, d], in_recv.at[c, z], (k, a, zt))
 
-    def relay():
-        return remote(following.at[:, :, rows_of(chunks - 1), :], relayed, relay_send, relay_recv, (k_up, a, z))
-
-    def homeward(c, d, target=None):
+    def relay(e):
+        return remote(
+            following.at[:, :, rows_of(kept + e), :], extra.at[:, :, rows_of(e), :],
+            relay_send.at[e], relay_recv.at[e], (k_up, a, z),
+        )
+
+    def homeward(c, d, extras=False):
         zt = lax.rem(z + d, nlon)
-        home = c if target is None else target
+        home = c - EXTRA if extras else c
         src = y_own.at[:, :, rows_of(c), pl.ds(pl.multiple_of(zt * width, width), width)]
         dst = out_hbm.at[:, pl.ds(z * per, per), rows_of(home), :]
-        if target is not None and d == 0:
+        if extras and d == 0:
             return local(src, dst, out_recv.at[home, z])
         return remote(
-            src, dst, out_send.at[c, d], out_recv.at[home, z], (k_up if target is None else k, a, zt)
+            src, dst, out_send.at[c, d], out_recv.at[home, z], (k if extras else k_up, a, zt)
         )
 
     order = list(range(1, nlon)) + [0]
@@ -182,6 +190,12 @@
     def _():
         for copy in own_copies(back_hbm):
             copy.start()
+
+    extra_copy = local(back_hbm.at[:, :, pl.ds(kept * CHUNK, EXTRA * CHUNK), :], extra, extra_sem)
+
+    @pl.when(k == 0)
+    def _():
+        extra_copy.start()
 
     waves_copy = local(waves_hbm, waves_ref, waves_sem)
     waves_copy.start()
@@ -266,6 +280,14 @@
                     side,
                 )
 
+    @pl.when(k == 0)
+    def _():
+        extra_copy.wait()
+
+        @pl.loop(0, fields)
+        def _(c):
+            extra[c] = own[c, :, pl.ds(kept * CHUNK, EXTRA * CHUNK), :] - extra[c]
+
     pl.semaphore_wait(barrier, nlon - 1 + 4 * nlon)
 
     @pl.when(k < last)
@@ -273,8 +295,20 @@
         for copy in pack_copies(0) + row_copies() + corner_copies() + pack_copies(1):
             copy.start()
 
-    for c in range(chunks):
+    for c in range(kept):
         next_copy(c).start()
+
+    @pl.when(k > 0)
+    def _():
+        for c in range(kept, chunks):
+            next_copy(c).start()
+
+    @pl.when(k == 0)
+    def _():
+        @pl.loop(0, EXTRA)
+        def _(e):
+            for d in order:
+                inward(chunks + e, d, True).start()
 
     def edge_blocks(numbers, corner):
         @pl.loop(0, fields)
@@ -468,18 +502,23 @@
             for d in order:
                 homeward(c, d).start()
 
-        @pl.when(c == chunks)
+        @pl.when(c >= chunks)
         def _():
             for d in order:
-                homeward(chunks, d, chunks - 1).start()
+                homeward(c, d, True).start()
 
     def send_defects(c):
         for d in order:
             inward(c, d).start()
 
+    def pass_on(e):
+        landed(extra.at[:, :, rows_of(e), :], relay_recv.at[e])
+        for d in order:
+            inward(chunks + e, d, True).start()
+
     @pl.when(k == last)
     def _():
-        @pl.loop(0, chunks)
+        @pl.loop(0, kept)
         def _(c):
             landed(following.at[:, :, rows_of(c), :], next_recv.at[c])
 
@@ -511,15 +550,19 @@
                             following[field, g, rows_of(c), cols] - state[field, j, at, :]
                         )
 
-            passes = (k == giver) & (c == chunks - 1)
+            passes = (k == giver) & (c >= kept)
 
             @pl.when(passes)
             def _():
-                relay().start()
+                relay(c - kept).start()
 
             @pl.when(jnp.logical_not(passes))
             def _():
                 send_defects(c)
+
+            @pl.when((k == taker) & (c > kept))
+            def _():
+                pass_on(c - kept - 1)
 
             @pl.when(c == 0)
             def _():
@@ -527,41 +570,56 @@
                 spread_scales()
                 waves_copy.wait()
 
-            @pl.when(c >= LAG)
-            def _():
-                filtered(c - LAG)
-
-    handled = chunks + (k == taker).astype(jnp.int32) - (k == giver).astype(jnp.int32)
-
-    @pl.loop(jnp.where(k == last, 0, chunks - LAG), handled)
+            @pl.loop(0, 2)
+            def _(turn):
+                slot = jnp.where(turn == 0, chunks + c, c - LAG)
+                begun = ((k == 0) & (c < EXTRA)).astype(jnp.int32)
+                ready = ((c >= LAG) & (c - LAG < n_own)).astype(jnp.int32)
+
+                @pl.when(jnp.where(turn == 0, begun, ready) == 1)
+                def _():
+                    filtered(slot)
+
+        @pl.when(k == taker)
+        def _():
+            pass_on(EXTRA - 1)
+
+    first_slot = jnp.where(k == last, 0, jnp.minimum(n_own, chunks - LAG))
+
+    @pl.loop(first_slot, n_own + EXTRA * is_taker)
     def _(c):
         filtered(c)
-
-        @pl.when((k == taker) & (c == chunks - LAG))
-        def _():
-            landed(relayed, relay_recv)
-            for d in order:
-                inward(chunks, d, relayed).start()
 
     @pl.loop(0, chunks)
     def _(c):
         for s in range(nlon):
             landed(out_hbm.at[:, pl.ds(s * per, per), rows_of(c), :], out_recv.at[c, s])
+
+    for c in range(kept):
         next_copy(c).wait_send()
 
-    @pl.loop(0, handled)
+    @pl.when(k > 0)
+    def _():
+        for c in range(kept, chunks):
+            next_copy(c).wait_send()
+
+    @pl.loop(0, n_own)
+    def _(c):
+        for d in range(nlon):
+            if d:
+                inward(c, d).wait_send()
+            homeward(c, d).wait_send()
+
+    @pl.loop(chunks, chunks + n_extra)
     def _(c):
         for d in range(1, nlon):
-            inward(c, d, relayed).wait_send()
-            homeward(c, d, 0).wait_send()
-
-        @pl.when(c < chunks)
-        def _():
-            homeward(c, 0).wait_send()
+            inward(c, d, True).wait_send()
+            homeward(c, d, True).wait_send()
 
     @pl.when(k == giver)
     def _():
-        relay().wait_send()
+        for e in range(EXTRA):
+            relay(e).wait_send()
 
     @pl.when(k < last)
     def _():
@@ -589,7 +647,7 @@
         corner_like = pltpu.VMEM((4, SUBLANES, LANES), f32)
         pack_like = pltpu.VMEM((2, fields, span // SUBLANES, SUBLANES, LANES), f32)
         rows_like = pltpu.VMEM((fields, ring, spread_rows, LANES), f32)
-        slab_like = pltpu.VMEM((fields, per, span + CHUNK, length), f32)
+        slab_like = pltpu.VMEM((fields, per, span + EXTRA * CHUNK, length), f32)
         out = pl.pallas_call(
             lambda *refs: kernel(nsub, nlat, nlon, *refs),
             name="weighted_defects",
@@ -606,14 +664,14 @@
                 pltpu.VMEM((fields, PAD, width), f32),
                 corner_like, corner_like, pack_like, pack_like,
                 pltpu.VMEM(natural, f32),
-                pltpu.VMEM((fields, SUBLANES, CHUNK, width), f32),
+                pltpu.VMEM((fields, SUBLANES, EXTRA * CHUNK, width), f32),
                 slab_like, slab_like,
                 rows_like, rows_like, rows_like,
-                dma, dma((fields,)),
+                dma, dma((fields,)), dma,
                 dma((2,)), dma((2,)), dma((4,)), dma((4,)), dma((2, 2)), dma((2, 2)),
-                dma((chunks,)), dma((chunks,)), dma, dma,
-                dma((chunks + 1, nlon)), dma((chunks + 1, nlon)),
-                dma((chunks + 1, nlon)), dma((chunks, nlon)),
+                dma((chunks,)), dma((chunks,)), dma((EXTRA,)), dma((EXTRA,)),
+                dma((chunks + EXTRA, nlon)), dma((chunks + EXTRA, nlon)),
+                dma((chunks + EXTRA, nlon)), dma((chunks, nlon)),
             ],
             compiler_params=pltpu.CompilerParams(collective_id=0, has_side_effects=True, vmem_limit_bytes=VMEM_LIMIT),
         )(

time: 87.5 us -> 82.2 us (0.939); the launches traced: 86.4 us -> 82 us
  Pallas kernels: 84.5 us -> 80.2 us
    pallas_call x1, Pallas kernels: 84.5 us -> 80.2 us  [shards(): pl.pallas_call(lambda *refs: kernel(nsub, nlat, nlon, *refs), name='weigh...]
where the time goes in v5:
time: 82.2 us; the launch traced here: 82 us
  Pallas kernels  80.2 us (98%)
  local copies, waits for them, and re-layouts  1.85 us (2%)
    pallas_call x1, Pallas kernels, shards(): pl.pallas_call(lambda *refs: kernel(nsub, nlat, nlon, *refs), name='weigh...  80.2 us
    unnamed x3, local copies, waits for them, and re-layouts  1.85 us

profile of v5, /device:TPU:1, one launch (start us, length us, event | category | flops | bytes accessed | tf_op | source)
XLA Modules:
  0.0 82.0 jit_solution(5316712046205825608)
XLA Ops:
  0.0 0.0 copy-start
  0.0 0.7 copy-done
  0.7 80.2 %weighted_defects.1 = f32[3,8,64,256]{3,2,1,0:T(8,128)S(1)} custom-call(f32[3,8,64,256]{3,2,1,0:T(8,128)} %bitcast.4, f32[3,8,64,256]{3,2,1,0:T(8,128)} %bitcast.5, f32[3,513]{1,0:T(4,128)S(1)} %copy-done, bf16[2,2,768,512]{3,2,1,0:T(8,128)(2,1)} %constant.2.clone.refs_3_), custom_call_target="tpu_custom_call" | custom-call | tf_op jit(solution)/shard_map/weighted_defects/pallas_call | solution.py:651
  80.9 1.1 %copy.6 = f32[1,3,512,256]{3,2,1,0:T(8,128)} copy(f32[1,3,512,256]{3,2,1,0:T(8,128)S(1)} %bitcast.3) | data formatting | bytes 3145728
Async XLA Ops:
  0.0 0.7 copy-start

commit v6 on v5

--- a/solution.py
+++ b/solution.py
@@ -8,7 +8,7 @@
 
 STEPS = 3
 PAD = 16
-EDGE = 16
+EDGE = 3 * STEPS
 SUBLANES = 8
 LANES = 128
 CHUNK = 8
@@ -51,11 +51,11 @@
 
 
 def kernel(
-    nsub, nlat, nlon, x_hbm, back_hbm, w_ref, waves_hbm, out_hbm,
-    waves_ref, wpad, scales, frows, own, top, bot, corners,
+    nsub, nlat, nlon, x_hbm, back_hbm, w_hbm, waves_hbm, out_hbm,
+    waves_ref, w_ref, wpad, scales, frows, own, top, bot, corners,
     corner_packs, packed, got_packed, following, extra, slab, y_own, state, mid1, mid2,
-    waves_sem, own_sem, extra_sem, rows_send, rows_recv, corner_send, corner_recv,
-    pack_send, pack_recv, next_send, next_recv, relay_send, relay_recv, in_send, in_recv, out_send, out_recv,
+    waves_sem, w_sem, own_sem, extra_sem, rows_send, rows_recv, corner_send, corner_recv,
+    pack_send, pack_recv, next_send, next_recv, part_send, part_recv, relay_send, relay_recv, in_send, in_recv, out_send, out_recv,
 ):
     k = lax.axis_index("sub")
     a = lax.axis_index("lat")
@@ -88,9 +88,10 @@
         pl.semaphore_signal(
             barrier, inc=1, device_id=(k, a, lax.rem(z + d, nlon)), device_id_type=MESH
         )
-    for d in range(nlon):
-        for there in ((k, a_up), (k, a_down), (k_up, a), (k_down, a)):
-            pl.semaphore_signal(barrier, inc=1, device_id=there + (jnp.int32(d),), device_id_type=MESH)
+    for there in ((k_up, a, z), (k_down, a, z)) + tuple(
+        (k, lat, lon) for lat in (a_up, a_down) for lon in (z_down, z, z_up)
+    ):
+        pl.semaphore_signal(barrier, inc=1, device_id=there, device_id_type=MESH)
 
     mine = pl.ds(pl.multiple_of(z * width, width), width)
 
@@ -125,14 +126,16 @@
         ]
 
     blocks_of_span = span // SUBLANES
-    early = blocks_of_span // 2 + 1
     turn = PAD // SUBLANES
-
-    def place_of(i):
-        return (i + turn) % blocks_of_span
+    slots = LANES // EDGE
+    first_blocks = list(range(turn + 1)) + list(range(blocks_of_span - turn, blocks_of_span))
+    other_blocks = [i for i in range(blocks_of_span) if i not in first_blocks]
+    early, late = [[(i, g) for i in numbers for g in range(SUBLANES)] for numbers in (first_blocks, other_blocks)]
+    n_early, n_late = pl.cdiv(len(early), slots), pl.cdiv(len(late), slots)
+    packs = ((early, 0), (late, n_early))
 
     def pack_copies(part):
-        at = pl.ds(0, early) if part == 0 else pl.ds(early, blocks_of_span - early)
+        at = pl.ds(0, n_early) if part == 0 else pl.ds(n_early, n_late)
         return [
             remote(
                 packed.at[i, :, at], got_packed.at[i, :, at],
@@ -148,6 +151,12 @@
         return remote(
             x_hbm.at[:, :, rows_of(c), :], following.at[:, :, rows_of(c), :],
             next_send.at[c], next_recv.at[c], (k_down, a, z),
+        )
+
+    def part_copy(c, d):
+        block = (slice(None), pl.ds(lax.rem(z + d, nlon) * per, per), rows_of(c), slice(None))
+        return remote(
+            x_hbm.at[block], following.at[block], part_send.at[c, d], part_recv.at[c, d], (k_down, a, z)
         )
 
     def inward(c, d, extras=False):
@@ -198,7 +207,6 @@
         extra_copy.start()
 
     waves_copy = local(waves_hbm, waves_ref, waves_sem)
-    waves_copy.start()
 
     lane = lax.broadcasted_iota(jnp.int32, (SUBLANES, LANES), 1)
 
@@ -265,9 +273,12 @@
         def _(c):
             for side in range(2):
                 cols = pl.ds(0 if side == 0 else width - LANES, LANES)
-                whole = merge([own[c, g, :, cols] for g in range(SUBLANES)], side)
-                for i in range(blocks_of_span):
-                    packed[side, c, place_of(i)] = whole[SUBLANES * i : SUBLANES * (i + 1)]
+                for blocks, base in packs:
+                    for v in range(0, len(blocks), slots):
+                        packed[side, c, base + v // slots] = merge(
+                            [own[c, g, pl.ds(SUBLANES * i, SUBLANES), cols] for i, g in blocks[v : v + slots]],
+                            side,
+                        )
 
         for i, (g, first) in enumerate(ends):
             for side in range(2):
@@ -288,19 +299,22 @@
         def _(c):
             extra[c] = own[c, :, pl.ds(kept * CHUNK, EXTRA * CHUNK), :] - extra[c]
 
-    pl.semaphore_wait(barrier, nlon - 1 + 4 * nlon)
+    pl.semaphore_wait(barrier, nlon - 1 + 8)
 
     @pl.when(k < last)
     def _():
         for copy in pack_copies(0) + row_copies() + corner_copies() + pack_copies(1):
             copy.start()
 
-    for c in range(kept):
-        next_copy(c).start()
+    @pl.when(k == 0)
+    def _():
+        for c in range(kept):
+            for d in order:
+                part_copy(c, d).start()
 
     @pl.when(k > 0)
     def _():
-        for c in range(kept, chunks):
+        for c in range(chunks):
             next_copy(c).start()
 
     @pl.when(k == 0)
@@ -310,22 +324,25 @@
             for d in order:
                 inward(chunks + e, d, True).start()
 
-    def edge_blocks(numbers, corner):
+    waves_copy.start()
+    w_copy = local(w_hbm, w_ref, w_sem)
+    w_copy.start()
+
+    def edge_blocks(blocks, base, corner):
         @pl.loop(0, fields)
         def _(c):
             def put(r, g, value):
                 state[c, groups, strided(r + PAD, g), :] = value
 
-            for i in numbers:
-                right, left = got_packed[0, c, place_of(i)], got_packed[1, c, place_of(i)]
-                for g in range(SUBLANES):
-                    value = join(right, left, g)
-                    r = SUBLANES * i
-                    put(r, g, value)
-                    if r >= span - PAD and g < SUBLANES - 1:
-                        put(r - span, g + 1, value)
-                    if r < PAD and g > 0:
-                        put(r + span, g - 1, value)
+            for n, (i, g) in enumerate(blocks):
+                v = base + n // slots
+                value = join(got_packed[0, c, v], got_packed[1, c, v], n % slots)
+                r = SUBLANES * i
+                put(r, g, value)
+                if r >= span - PAD and g < SUBLANES - 1:
+                    put(r - span, g + 1, value)
+                if r < PAD and g > 0:
+                    put(r + span, g - 1, value)
 
         for c in range(fields):
             for b in range(turn):
@@ -333,20 +350,17 @@
                 g, r = ((0, -PAD), (SUBLANES - 1, span))[corner]
                 state[c, groups, strided(r + SUBLANES * b + PAD, g), :] = value
 
-    early_blocks = [i for i in range(blocks_of_span) if place_of(i) < early]
-    late_blocks = [i for i in range(blocks_of_span) if place_of(i) >= early]
-
     def late_edges():
         for i in range(2):
-            landed(got_packed.at[i, :, pl.ds(early, blocks_of_span - early)], pack_recv.at[1, i])
+            landed(got_packed.at[i, :, pl.ds(n_early, n_late)], pack_recv.at[1, i])
             landed(corners.at[2 + i], corner_recv.at[2 + i])
-        edge_blocks(late_blocks, 1)
+        edge_blocks(late, n_early, 1)
 
     @pl.when(k < last)
     def _():
-        coriolis_rows()
         landed(top, rows_recv.at[0])
         landed(bot, rows_recv.at[1])
+        coriolis_rows()
 
         @pl.loop(0, fields)
         def _(c):
@@ -364,9 +378,9 @@
                 )
 
         for i in range(2):
-            landed(got_packed.at[i, :, pl.ds(0, early)], pack_recv.at[0, i])
+            landed(got_packed.at[i, :, pl.ds(0, n_early)], pack_recv.at[0, i])
             landed(corners.at[i], corner_recv.at[i])
-        edge_blocks(early_blocks, 0)
+        edge_blocks(early, 0, 0)
 
     @pl.when(k == last)
     def _():
@@ -375,6 +389,7 @@
 
     def spread_scales():
         wpad[...] = jnp.zeros_like(wpad)
+        w_copy.wait()
         wpad[0:fields, 0 : half + 1] = w_ref[...]
         depth = wpad.shape[1]
         parts, rest = [], wpad[...]
@@ -520,15 +535,13 @@
     def _():
         @pl.loop(0, kept)
         def _(c):
-            landed(following.at[:, :, rows_of(c), :], next_recv.at[c])
-
-            @pl.loop(0, fields)
-            def _(field):
-                following[field, :, rows_of(c), :] = (
-                    following[field, :, rows_of(c), :] - own[field, :, rows_of(c), :]
+            for d in order:
+                at = pl.ds(lax.rem(z + d, nlon) * per, per)
+                landed(following.at[:, at, rows_of(c), :], part_recv.at[c, d])
+                following[:, at, rows_of(c), :] = (
+                    following[:, at, rows_of(c), :] - own[:, at, rows_of(c), :]
                 )
-
-            send_defects(c)
+                inward(c, d).start()
 
         spread_scales()
         waves_copy.wait()
@@ -595,12 +608,15 @@
         for s in range(nlon):
             landed(out_hbm.at[:, pl.ds(s * per, per), rows_of(c), :], out_recv.at[c, s])
 
-    for c in range(kept):
-        next_copy(c).wait_send()
+    @pl.when(k == 0)
+    def _():
+        for c in range(kept):
+            for d in range(nlon):
+                part_copy(c, d).wait_send()
 
     @pl.when(k > 0)
     def _():
-        for c in range(kept, chunks):
+        for c in range(chunks):
             next_copy(c).wait_send()
 
     @pl.loop(0, n_own)
@@ -642,20 +658,23 @@
         f32, bf16 = jnp.float32, jnp.bfloat16
         dma = pltpu.SemaphoreType.DMA
         any_space = pl.BlockSpec(memory_space=pl.ANY)
-        vmem = pl.BlockSpec(memory_space=pltpu.VMEM)
         spread_rows = SUBLANES * (span + 2 * PAD)
         corner_like = pltpu.VMEM((4, SUBLANES, LANES), f32)
-        pack_like = pltpu.VMEM((2, fields, span // SUBLANES, SUBLANES, LANES), f32)
+        slots = LANES // EDGE
+        near = SUBLANES * (2 * (PAD // SUBLANES) + 1)
+        n_packs = pl.cdiv(near, slots) + pl.cdiv(span - near, slots)
+        pack_like = pltpu.VMEM((2, fields, n_packs, SUBLANES, LANES), f32)
         rows_like = pltpu.VMEM((fields, ring, spread_rows, LANES), f32)
         slab_like = pltpu.VMEM((fields, per, span + EXTRA * CHUNK, length), f32)
         out = pl.pallas_call(
             lambda *refs: kernel(nsub, nlat, nlon, *refs),
             name="weighted_defects",
             out_shape=jax.ShapeDtypeStruct(natural, f32),
-            in_specs=[any_space, any_space, vmem, any_space],
+            in_specs=[any_space, any_space, any_space, any_space],
             out_specs=any_space,
             scratch_shapes=[
                 pltpu.VMEM((2, 2, half + half // 2, half), bf16),
+                pltpu.VMEM((fields, half + 1), f32),
                 pltpu.VMEM((8, half + LANES), f32),
                 pltpu.VMEM((fields * per * CHUNK, length), f32),
                 pltpu.VMEM((spread_rows, LANES), f32),
@@ -667,15 +686,16 @@
                 pltpu.VMEM((fields, SUBLANES, EXTRA * CHUNK, width), f32),
                 slab_like, slab_like,
                 rows_like, rows_like, rows_like,
-                dma, dma((fields,)), dma,
+                dma, dma, dma((fields,)), dma,
                 dma((2,)), dma((2,)), dma((4,)), dma((4,)), dma((2, 2)), dma((2, 2)),
-                dma((chunks,)), dma((chunks,)), dma((EXTRA,)), dma((EXTRA,)),
+                dma((chunks,)), dma((chunks,)),
+                dma((chunks - EXTRA, nlon)), dma((chunks - EXTRA, nlon)), dma((EXTRA,)), dma((EXTRA,)),
                 dma((chunks + EXTRA, nlon)), dma((chunks + EXTRA, nlon)),
                 dma((chunks + EXTRA, nlon)), dma((chunks, nlon)),
             ],
             compiler_params=pltpu.CompilerParams(collective_id=0, has_side_effects=True, vmem_limit_bytes=VMEM_LIMIT),
         )(
-            launch.reshape(natural), backdrop.reshape(natural), inverse_variances,
+            launch.reshape(natural), backdrop.reshape(natural), pltpu.with_memory_space_constraint(inverse_variances, pltpu.HBM),
             jnp.asarray(waves(length)),
         )
         return out.reshape(launch.shape)

time: 82.2 us -> 81.2 us (0.988)
  Pallas kernels: 80.2 us -> 79.1 us
    pallas_call x1, Pallas kernels: 80.2 us -> 79.1 us  [shards(): pl.pallas_call(lambda *refs: kernel(nsub, nlat, nlon, *refs), name='weigh...]
    unnamed x3 -> x1, local copies, waits for them, and re-layouts: 1.85 us -> 1.15 us
where the time goes in v6:
time: 81.2 us; the launch traced here: 80.2 us
  Pallas kernels  79.1 us (97%)
  local copies, waits for them, and re-layouts  1.15 us (1%)
    pallas_call x1, Pallas kernels, shards(): pl.pallas_call(lambda *refs: kernel(nsub, nlat, nlon, *refs), name='weigh...  79.1 us

profile of v6, /device:TPU:1, one launch (start us, length us, event | category | flops | bytes accessed | tf_op | source)
XLA Modules:
  0.0 80.2 jit_solution(2809979562104851166)
XLA Ops:
  0.0 79.1 %weighted_defects.1 = f32[3,8,64,256]{3,2,1,0:T(8,128)S(1)} custom-call(f32[3,8,64,256]{3,2,1,0:T(8,128)} %bitcast.4, f32[3,8,64,256]{3,2,1,0:T(8,128)} %bitcast.5, f32[3,513]{1,0:T(4,128)} %refs_2_.1, bf16[2,2,768,512]{3,2,1,0:T(8,128)(2,1)} %constant.2.clone.refs_3_), custom_call_target="tpu_custom_call" | custom-call | tf_op jit(solution)/shard_map/weighted_defects/pallas_call | solution.py:669
  79.1 1.1 %copy.6 = f32[1,3,512,256]{3,2,1,0:T(8,128)} copy(f32[1,3,512,256]{3,2,1,0:T(8,128)S(1)} %bitcast.3) | data formatting | bytes 3145728

commit v7 on v6

--- a/solution.py
+++ b/solution.py
@@ -14,7 +14,7 @@
 CHUNK = 8
 BLOCK = 4
 LAG = 3
-EXTRA = 5
+EXTRA = 4
 VMEM_LIMIT = 52 * 2**20
 MESH = pl.DeviceIdType.MESH
 
@@ -303,7 +303,7 @@
 
     @pl.when(k < last)
     def _():
-        for copy in pack_copies(0) + row_copies() + corner_copies() + pack_copies(1):
+        for copy in pack_copies(0) + row_copies() + corner_copies():
             copy.start()
 
     @pl.when(k == 0)
@@ -323,6 +323,11 @@
         def _(e):
             for d in order:
                 inward(chunks + e, d, True).start()
+
+    @pl.when(k < last)
+    def _():
+        for copy in pack_copies(1):
+            copy.start()
 
     waves_copy.start()
     w_copy = local(w_hbm, w_ref, w_sem)

time: 81.2 us -> 80.5 us (level)
  no operation moved by 1% of the time
where the time goes in v7:
time: 80.5 us; the launch traced here: 80.3 us
  Pallas kernels  79.2 us (98%)
  local copies, waits for them, and re-layouts  1.15 us (1%)
    pallas_call x1, Pallas kernels, shards(): pl.pallas_call(lambda *refs: kernel(nsub, nlat, nlon, *refs), name='weigh...  79.2 us

profile of v7, /device:TPU:1, one launch (start us, length us, event | category | flops | bytes accessed | tf_op | source)
XLA Modules:
  0.0 80.3 jit_solution(9161755488228080080)
XLA Ops:
  0.0 79.2 %weighted_defects.1 = f32[3,8,64,256]{3,2,1,0:T(8,128)S(1)} custom-call(f32[3,8,64,256]{3,2,1,0:T(8,128)} %bitcast.4, f32[3,8,64,256]{3,2,1,0:T(8,128)} %bitcast.5, f32[3,513]{1,0:T(4,128)} %refs_2_.1, bf16[2,2,768,512]{3,2,1,0:T(8,128)(2,1)} %constant.2.clone.refs_3_), custom_call_target="tpu_custom_call" | custom-call | tf_op jit(solution)/shard_map/weighted_defects/pallas_call | solution.py:674
  79.2 1.1 %copy.6 = f32[1,3,512,256]{3,2,1,0:T(8,128)} copy(f32[1,3,512,256]{3,2,1,0:T(8,128)S(1)} %bitcast.3) | data formatting | bytes 3145728

commit v8 on v7

--- a/solution.py
+++ b/solution.py
@@ -608,11 +608,6 @@
     def _(c):
         filtered(c)
 
-    @pl.loop(0, chunks)
-    def _(c):
-        for s in range(nlon):
-            landed(out_hbm.at[:, pl.ds(s * per, per), rows_of(c), :], out_recv.at[c, s])
-
     @pl.when(k == 0)
     def _():
         for c in range(kept):
@@ -646,6 +641,11 @@
     def _():
         for copy in row_copies() + corner_copies() + pack_copies(0) + pack_copies(1):
             copy.wait_send()
+
+    @pl.loop(0, chunks)
+    def _(c):
+        for s in range(nlon):
+            landed(out_hbm.at[:, pl.ds(s * per, per), rows_of(c), :], out_recv.at[c, s])
 
 
 def solution(mesh):

time: 80.5 us -> 80.4 us (level)
  no operation moved by 1% of the time
where the time goes in v8:
time: 80.4 us; the launch traced here: 80.2 us
  Pallas kernels  79.1 us (98%)
  local copies, waits for them, and re-layouts  1.15 us (1%)
    pallas_call x1, Pallas kernels, shards(): pl.pallas_call(lambda *refs: kernel(nsub, nlat, nlon, *refs), name='weigh...  79.1 us

profile of v8, /device:TPU:1, one launch (start us, length us, event | category | flops | bytes accessed | tf_op | source)
XLA Modules:
  0.0 80.2 jit_solution(795544684298454838)
XLA Ops:
  0.0 79.1 %weighted_defects.1 = f32[3,8,64,256]{3,2,1,0:T(8,128)S(1)} custom-call(f32[3,8,64,256]{3,2,1,0:T(8,128)} %bitcast.4, f32[3,8,64,256]{3,2,1,0:T(8,128)} %bitcast.5, f32[3,513]{1,0:T(4,128)} %refs_2_.1, bf16[2,2,768,512]{3,2,1,0:T(8,128)(2,1)} %constant.2.clone.refs_3_), custom_call_target="tpu_custom_call" | custom-call | tf_op jit(solution)/shard_map/weighted_defects/pallas_call | solution.py:674
  79.1 1.1 %copy.6 = f32[1,3,512,256]{3,2,1,0:T(8,128)} copy(f32[1,3,512,256]{3,2,1,0:T(8,128)S(1)} %bitcast.3) | data formatting | bytes 3145728

commit v9 on v8

--- a/solution.py
+++ b/solution.py
@@ -185,7 +185,7 @@
             src, dst, out_send.at[c, d], out_recv.at[home, z], (k if extras else k_up, a, zt)
         )
 
-    order = list(range(1, nlon)) + [0]
+    order = sorted(range(1, nlon), key=lambda d: -min(d, nlon - d)) + [0]
 
     def own_copies(src):
         return [local(src.at[c], own.at[c], own_sem.at[c]) for c in range(fields)]

time: 80.4 us -> 80.4 us (level)
  no operation moved by 1% of the time
where the time goes in v9:
time: 80.4 us; the launch traced here: 80.3 us
  Pallas kernels  79.1 us (98%)
  local copies, waits for them, and re-layouts  1.15 us (1%)
    pallas_call x1, Pallas kernels, shards(): pl.pallas_call(lambda *refs: kernel(nsub, nlat, nlon, *refs), name='weigh...  79.1 us

profile of v9, /device:TPU:1, one launch (start us, length us, event | category | flops | bytes accessed | tf_op | source)
XLA Modules:
  0.0 80.3 jit_solution(12779640449668333040)
XLA Ops:
  0.0 79.1 %weighted_defects.1 = f32[3,8,64,256]{3,2,1,0:T(8,128)S(1)} custom-call(f32[3,8,64,256]{3,2,1,0:T(8,128)} %bitcast.4, f32[3,8,64,256]{3,2,1,0:T(8,128)} %bitcast.5, f32[3,513]{1,0:T(4,128)} %refs_2_.1, bf16[2,2,768,512]{3,2,1,0:T(8,128)(2,1)} %constant.2.clone.refs_3_), custom_call_target="tpu_custom_call" | custom-call | tf_op jit(solution)/shard_map/weighted_defects/pallas_call | solution.py:674
  79.1 1.1 %copy.6 = f32[1,3,512,256]{3,2,1,0:T(8,128)} copy(f32[1,3,512,256]{3,2,1,0:T(8,128)S(1)} %bitcast.3) | data formatting | bytes 3145728
